TPU v7x, 32 devices: a whole 2x2x4 slice. The times are simulated.
32 devices in a mesh: tile: 8 (over z, x), slab: 4 (over y, core).
Axes of the slice: x: 2, y: 2, z: 4, core: 2. Of those that a mesh axis runs over, the one named last changes fastest.
Arguments:
- object_field: float32 [2, 2, 4096, 2048], P(None, None, 'tile', 'slab')
- probe: float32 [2, 256, 256], replicated, may hold values from -5 to 5
- kernel_phase: float32 [256, 256], replicated, may hold values from -3.140625 to 3.140625
- measured: float32 [128, 256, 256], P(('tile', 'slab')), may hold values from 0.2 to 2
- positions: int32 [128, 2], P(('tile', 'slab')), may hold values from 0 to 3840, as said below
- batch: int32 [128], P(('tile', 'slab')), may hold values from 0 to 1
Outputs:
- object_new: float32 [2, 2, 4096, 2048], P(None, None, 'tile', 'slab')
- probe_new: float32 [2, 256, 256], replicated
Inputs may be any that keep to these rules, and one draw needn't show every extreme that they name: `positions`: frame f's top-left pixel lies in the tile of rows t * 512 .. (t + 1) * 512 - 1 and columns s * 512 .. (s + 1) * 512 - 1, where t = (f // 4) // 4 and s = (f // 4) % 4; every frame lies inside the object.
All inputs are finite; a program needn't handle non-finite values.
Results may differ from a plain program's by a relative error of at most 0.0003.
Values sent between devices are 32-bit elements; how exact they have to be, the bound alone decides.
No kernel may reach another device: no remote copies, remote signals or barrier semaphores. Data moves between devices by JAX's collectives and lax.ppermute only.
A program may use at most 192 MiB of HBM per device.

v0:
```python
import math

import jax
import jax.numpy as jnp
import numpy as np
from jax import lax
from jax.experimental import pallas as pl
from jax.experimental.pallas import tpu as pltpu
from jax.sharding import PartitionSpec as P


BATCHES = 2
LANES = 128


def shifted(value, axis, steps):
    count = lax.axis_size(axis)
    first, last = (max(0, -steps), min(count, count - steps))
    return lax.ppermute(value, axis, [(source, source + steps) for source in range(first, last)])


def swapped(value, axis, step):
    count = lax.axis_size(axis)
    return lax.ppermute(value, axis, [(source, source ^ step) for source in range(count)])


def split_parts(table):
    high = table.astype(jnp.bfloat16)
    low = (table - high.astype(np.float32).astype(np.float64)).astype(jnp.bfloat16)
    return (high, low)


def dft_tables(side):
    half = side // 2
    index = np.arange(half)
    angle = 2.0 * math.pi * (index[:, None] * index[None, :] % half) / half
    cos, sin = (np.cos(angle) / math.sqrt(side), np.sin(angle) / math.sqrt(side))
    fore = np.block([[cos, -sin], [sin, cos]])
    back = np.block([[cos, sin], [-sin, cos]])
    fore_high, fore_low = split_parts(fore)
    back_high, back_low = split_parts(back)
    right = np.stack([np.concatenate([h, l], axis=0) for h, l in ((fore_high, fore_low), (back_high, back_low))])
    left = np.stack([np.concatenate([h, l], axis=1) for h, l in ((back_high, back_low), (fore_high, fore_low))])
    turn = 2.0 * math.pi * index / side
    twist = np.stack([np.cos(turn), -np.sin(turn)]).astype(np.float32)
    lane_twist = np.broadcast_to(twist[:, None, :], (2, 8, half))
    row_twist = np.broadcast_to(twist[:, :, None], (2, half, LANES))
    return tuple(jnp.asarray(np.ascontiguousarray(item)) for item in (right, left, lane_twist, row_twist))


def parts_of(value):
    high = value.astype(jnp.bfloat16)
    return (high, (value - high.astype(jnp.float32)).astype(jnp.bfloat16))


def dot(left, right):
    return jnp.dot(left, right, preferred_element_type=jnp.float32)


def by_rows(lead, table):
    high, low = parts_of(lead)
    side = table.shape[0] // 2
    table = jnp.concatenate([table[:side], table], axis=0)
    return dot(jnp.concatenate([high, low, high], axis=1), table)


def by_columns(table, lead):
    high, low = parts_of(lead)
    side = table.shape[1] // 2
    table = jnp.concatenate([table[:, :side], table], axis=1)
    return dot(table, jnp.concatenate([high, low, high], axis=0))


def lanes_forward(real, imag, table, twist):
    half = real.shape[1] // 2
    rows = real.shape[0]
    cos, sin = (twist[0, 0:1, :], twist[1, 0:1, :])
    sum_real, sum_imag = (real[:, :half] + real[:, half:], imag[:, :half] + imag[:, half:])
    gap_real, gap_imag = (real[:, :half] - real[:, half:], imag[:, :half] - imag[:, half:])
    odd_real, odd_imag = (gap_real * cos - gap_imag * sin, gap_real * sin + gap_imag * cos)
    lead = jnp.concatenate(
        [jnp.concatenate([sum_real, sum_imag], axis=1), jnp.concatenate([odd_real, odd_imag], axis=1)], axis=0
    )
    out = by_rows(lead, table)
    even, odd = (out[:rows], out[rows:])
    return (
        jnp.concatenate([even[:, :half], odd[:, :half]], axis=1),
        jnp.concatenate([even[:, half:], odd[:, half:]], axis=1),
    )


def lanes_inverse(real, imag, table, twist):
    half = real.shape[1] // 2
    rows = real.shape[0]
    cos, sin = (twist[0, 0:1, :], twist[1, 0:1, :])
    lead = jnp.concatenate(
        [
            jnp.concatenate([real[:, :half], imag[:, :half]], axis=1),
            jnp.concatenate([real[:, half:], imag[:, half:]], axis=1),
        ],
        axis=0,
    )
    out = by_rows(lead, table)
    even_real, even_imag = (out[:rows, :half], out[:rows, half:])
    odd_real, odd_imag = (out[rows:, :half], out[rows:, half:])
    turn_real, turn_imag = (odd_real * cos + odd_imag * sin, odd_imag * cos - odd_real * sin)
    return (
        jnp.concatenate([even_real + turn_real, even_real - turn_real], axis=1),
        jnp.concatenate([even_imag + turn_imag, even_imag - turn_imag], axis=1),
    )


def wide(twist, width):
    return jnp.concatenate([twist] * (width // twist.shape[1]), axis=1)


def rows_forward(real, imag, table, twist):
    half = real.shape[0] // 2
    cos, sin = (wide(twist[0], real.shape[1]), wide(twist[1], real.shape[1]))
    sum_real, sum_imag = (real[:half] + real[half:], imag[:half] + imag[half:])
    gap_real, gap_imag = (real[:half] - real[half:], imag[:half] - imag[half:])
    odd_real, odd_imag = (gap_real * cos - gap_imag * sin, gap_real * sin + gap_imag * cos)
    even = by_columns(table, jnp.concatenate([sum_real, sum_imag], axis=0))
    odd = by_columns(table, jnp.concatenate([odd_real, odd_imag], axis=0))
    return (
        jnp.concatenate([even[:half], odd[:half]], axis=0),
        jnp.concatenate([even[half:], odd[half:]], axis=0),
    )


def rows_inverse(real, imag, table, twist):
    half = real.shape[0] // 2
    cos, sin = (wide(twist[0], real.shape[1]), wide(twist[1], real.shape[1]))
    even = by_columns(table, jnp.concatenate([real[:half], imag[:half]], axis=0))
    odd = by_columns(table, jnp.concatenate([real[half:], imag[half:]], axis=0))
    odd_real, odd_imag = (odd[:half], odd[half:])
    turn_real, turn_imag = (odd_real * cos + odd_imag * sin, odd_imag * cos - odd_real * sin)
    return (
        jnp.concatenate([even[:half] + turn_real, even[:half] - turn_real], axis=0),
        jnp.concatenate([even[half:] + turn_imag, even[half:] - turn_imag], axis=0),
    )


CHUNK = 128


def chain(load, middle, store, side, work, right, left, lane_twist, row_twist):
    for start in range(0, side, CHUNK):
        rows = slice(start, start + CHUNK)
        real, imag = lanes_forward(*load(rows), right[0], lane_twist)
        work[0, rows, :] = real
        work[1, rows, :] = imag
    real, imag = rows_forward(work[0], work[1], left[0], row_twist)
    real, imag = middle(real, imag)
    real, imag = rows_inverse(real, imag, left[1], row_twist)
    work[0] = real
    work[1] = imag

    for start in range(0, side, CHUNK):
        rows = slice(start, start + CHUNK)
        store(rows, *lanes_inverse(work[0, rows, :], work[1, rows, :], right[1], lane_twist))


STRIP = 64
ROWS = 8


def numbers(groups, axis):
    return lax.broadcasted_iota(jnp.int32, (groups, ROWS, LANES), axis)


def bases(at, step):
    base = pl.multiple_of(at // step * step, step)
    return (base, at - base)


def cut(field, target, row, col, side):
    left, right = bases(col, LANES)
    top, under = bases(row, ROWS)
    groups = STRIP // ROWS
    take_rows = numbers(groups, 1) < ROWS - under
    take_cols = numbers(groups, 2) < LANES - right
    up, back = (lax.rem(ROWS - under, ROWS), lax.rem(LANES - right, LANES))

    def read(part, down, k):
        at = (part, pl.ds(pl.multiple_of(top + down, ROWS), STRIP + ROWS), pl.ds(pl.multiple_of(left + k * LANES, LANES), LANES))
        value = pltpu.roll(field[at], back, 1).reshape(groups + 1, ROWS, LANES)
        value = pltpu.roll(value, up, 1)
        return jnp.where(take_rows, value[:groups], value[1:])

    for part in range(field.shape[0]):

        @pl.loop(0, side // STRIP)
        def _(step):
            down = pl.multiple_of(step * STRIP, STRIP)
            turned = [read(part, down, k) for k in range(side // LANES + 1)]
            for k in range(side // LANES):
                value = jnp.where(take_cols, turned[k], turned[k + 1])
                target[part, pl.ds(down, STRIP), k * LANES : (k + 1) * LANES] = value.reshape(STRIP, LANES)


def place(field, source, row, col, side):
    left, right = bases(col, LANES)
    top, under = bases(row, ROWS)
    groups = STRIP // ROWS
    keep_rows = numbers(groups + 1, 1) >= under
    keep_cols = numbers(groups + 1, 2) >= right
    count = side // LANES
    edge = jnp.zeros((1, ROWS, LANES), jnp.float32)
    blank = jnp.zeros((groups + 1, ROWS, LANES), jnp.float32)

    def read(part, down, k):
        value = pltpu.roll(source[part, pl.ds(down, STRIP), k * LANES : (k + 1) * LANES], right, 1)
        value = pltpu.roll(value.reshape(groups, ROWS, LANES), under, 1)
        return jnp.where(
            keep_rows, jnp.concatenate([value, edge], axis=0), jnp.concatenate([edge, value], axis=0)
        )

    for part in range(field.shape[0]):

        @pl.loop(0, side // STRIP)
        def _(step):
            down = pl.multiple_of(step * STRIP, STRIP)
            turned = [blank] + [read(part, down, k) for k in range(count)] + [blank]
            for k in range(count + 1):
                value = jnp.where(keep_cols, turned[k + 1], turned[k]).reshape(STRIP + ROWS, LANES)
                spot = (
                    part,
                    pl.ds(pl.multiple_of(top + down, ROWS), STRIP + ROWS),
                    pl.ds(pl.multiple_of(left + k * LANES, LANES), LANES),
                )
                field[spot] = field[spot] + value


def halo_spans(side, rows, cols):
    return [
        (0, cols, side, side),
        (side, cols, rows - side, side),
        (rows, 0, side, side),
        (rows, side, side, cols - side),
        (rows, cols, side, side),
    ]


def own_spans(side, rows, cols):
    rest_rows, rest_cols = (rows - side, cols - side)
    return [
        (0, 0, side, side),
        (0, side, side, rest_cols),
        (side, 0, rest_rows, side),
        (side, side, rest_rows, rest_cols),
    ]


def grad_spans(side, rows, cols):
    return own_spans(side, rows, cols) + [
        (0, cols, rows, side),
        (rows, side, side, cols - side),
        (rows, 0, side, side),
        (rows, cols, side, side),
    ]


def copies(blocks, field, spans, sem, outward):
    made = []
    for block, (row, col, rows, cols) in zip(blocks, spans):
        window = field.at[:, pl.ds(row, rows), pl.ds(col, cols)]
        source, target = (window, block) if outward else (block, window)
        made.append(pltpu.make_async_copy(source, target, sem.at[len(made)]))
    return made


def start_all(items):
    for item in items:
        item.start()


def wait_all(items):
    for item in items:
        item.wait()


def clear(field):
    rows = field.shape[1]

    @pl.loop(0, rows // 16)
    def _(step):
        at = pl.ds(pl.multiple_of(step * 16, 16), 16)
        for part in range(field.shape[0]):
            field[part, at, :] = jnp.zeros((16, field.shape[2]), jnp.float32)


def three_parts(value, axis):
    high = value.astype(jnp.bfloat16)
    rest = value - high.astype(jnp.float32)
    mid = rest.astype(jnp.bfloat16)
    low = (rest - mid.astype(jnp.float32)).astype(jnp.bfloat16)
    return jnp.concatenate([high, mid, low], axis=axis)


def even_odd(value):
    side = value.shape[0]
    first, second = (lax.broadcasted_iota(jnp.int32, (side, side), axis) for axis in (0, 1))

    def table(source, target):
        at = jnp.where(target < side // 2, 2 * target, 2 * target - side + 1)
        return jnp.where(source == at, 1.0, 0.0).astype(jnp.bfloat16)

    right, left = (table(first, second), table(second, first))
    value = dot(three_parts(value, 1), jnp.concatenate([right] * 3, axis=0))
    return dot(jnp.concatenate([left] * 3, axis=1), three_parts(value, 0))


def sort_kernel(side, slots, number, measured, angle, amplitude, phase):
    turned = even_odd(angle[...])
    phase[0] = jnp.cos(turned)
    phase[1] = jnp.sin(turned)

    @pl.loop(0, slots)
    def _(slot):
        amplitude[slot] = even_odd(measured[slot])


def sources(refs, spans, layer):
    if len(refs) < len(spans):
        tile = refs[0].at[:, layer]
        return ([tile, *refs[1:]], [(0, 0, *tile.shape[1:]), *spans[4:]])
    return (refs, spans)


def first_kernel(spans, side, slots, number, *refs):
    at, which, probe, phase, right, left, lane_twist, row_twist = refs[:8]
    patches, incoming, field, work, sem = refs[-5:]
    blocks, places = sources(refs[8:-5], spans, 0)
    moves = copies(blocks, field, places, sem, False)
    start_all(moves)
    wait_all(moves)

    @pl.loop(0, slots)
    def _(slot):
        @pl.when(which[slot] == number)
        def _():
            patch = patches.at[slot]
            out = incoming.at[slot]
            cut(field, patch, at[slot, 0], at[slot, 1], side)

            def load(rows):
                real, imag = (patch[0, rows, :], patch[1, rows, :])
                return (
                    probe[0, rows, :] * real - probe[1, rows, :] * imag,
                    probe[0, rows, :] * imag + probe[1, rows, :] * real,
                )

            def middle(real, imag):
                return (real * phase[0] - imag * phase[1], real * phase[1] + imag * phase[0])

            def store(rows, real, imag):
                out[0, rows, :] = real
                out[1, rows, :] = imag

            chain(load, middle, store, side, work, right, left, lane_twist, row_twist)


def second_kernel(spans, side, slots, number, *refs):
    at, which, probe, phase, patches, incoming_all, measured, right, left, lane_twist, row_twist = refs[:11]
    sums, *grads = refs[-18:-9]
    field, total1, total0, patch, delta, behind_all, work, sem, sem_out = refs[-9:]
    rows, cols = (total0.shape[1] - side, total0.shape[2] - side)
    places_out = grad_spans(side, rows, cols)
    blocks, places = sources(refs[11:-18], spans, 1)
    moves = copies(blocks, field, places, sem, False)
    start_all(moves)
    clear(total1)
    clear(total0)
    sums[...] = jnp.zeros_like(sums)
    wait_all(moves)

    @pl.loop(0, slots)
    def _(slot):
        @pl.when(which[slot] == number)
        def _():
            incoming = incoming_all.at[slot]
            out = behind_all.at[slot]
            cut(field, patch, at[slot, 0], at[slot, 1], side)

            def load(rows):
                real, imag = (patch[0, rows, :], patch[1, rows, :])
                in_real, in_imag = (incoming[0, rows, :], incoming[1, rows, :])
                return (real * in_real - imag * in_imag, real * in_imag + imag * in_real)

            def middle(real, imag):
                power = real * real + imag * imag
                factor = 1.0 - measured[slot] * lax.rsqrt(jnp.maximum(power, 0.01))
                return (real * factor, imag * factor)

            def store(rows, real, imag):
                in_real, in_imag = (incoming[0, rows, :], incoming[1, rows, :])
                delta[0, rows, :] = in_real * real + in_imag * imag
                delta[1, rows, :] = in_real * imag - in_imag * real
                own_real, own_imag = (patch[0, rows, :], patch[1, rows, :])
                out[0, rows, :] = own_real * real + own_imag * imag
                out[1, rows, :] = own_real * imag - own_imag * real

            chain(load, middle, store, side, work, right, left, lane_twist, row_twist)
            place(total1, delta, at[slot, 0], at[slot, 1], side)

    moves1 = copies([grad.at[1] for grad in grads], total1, places_out, sem, True)
    start_all(moves1)

    @pl.loop(0, slots)
    def _(slot):
        @pl.when(which[slot] == number)
        def _():
            behind = behind_all.at[slot]
            first = patches.at[slot]

            def load(rows):
                return (behind[0, rows, :], behind[1, rows, :])

            def middle(real, imag):
                return (real * phase[0] + imag * phase[1], imag * phase[0] - real * phase[1])

            def store(rows, real, imag):
                in_real, in_imag = (probe[0, rows, :], probe[1, rows, :])
                delta[0, rows, :] = in_real * real + in_imag * imag
                delta[1, rows, :] = in_real * imag - in_imag * real
                own_real, own_imag = (first[0, rows, :], first[1, rows, :])
                sums[0, rows, :] = sums[0, rows, :] + (own_real * real + own_imag * imag)
                sums[1, rows, :] = sums[1, rows, :] + (own_real * imag - own_imag * real)
                sums[2, rows, :] = sums[2, rows, :] + (own_real * own_real + own_imag * own_imag)

            chain(load, middle, store, side, work, right, left, lane_twist, row_twist)
            place(total0, delta, at[slot, 0], at[slot, 1], side)

    moves0 = copies([grad.at[0] for grad in grads], total0, places_out, sem_out, True)
    start_all(moves0)
    wait_all(moves1)
    wait_all(moves0)


VMEM = pltpu.MemorySpace.VMEM
SMEM = pltpu.MemorySpace.SMEM
ANY = pl.ANY


def spec(space):
    return pl.BlockSpec(memory_space=space)


def f32(*shape):
    return jax.ShapeDtypeStruct(shape, jnp.float32)


def quarters(field, side):
    return (
        field[:, :side, :side],
        field[:, :side, side:],
        field[:, side:, :side],
        field[:, side:, side:],
    )


def surroundings(own):
    low_left = shifted(own[0], "tile", -1)
    corner = shifted(low_left, "slab", -1)
    low_right = shifted(own[1], "tile", -1)
    top = shifted(own[0], "slab", -1)
    mid = shifted(own[2], "slab", -1)
    return [top, mid, low_left, low_right, corner]


def gathered(grads):
    low_right = shifted(grads[5], "tile", 1)
    corner = shifted(grads[7], "slab", 1)
    right = shifted(grads[4], "slab", 1)
    side = corner.shape[2]
    layers = []
    for layer in range(corner.shape[0]):
        low_left = shifted(grads[6][layer] + corner[layer], "tile", 1)
        layers.append(
            (
                grads[0][layer] + right[layer, :, :side] + low_left,
                grads[1][layer] + low_right[layer],
                grads[2][layer] + right[layer, :, side:],
                grads[3][layer],
            )
        )
    return layers


def stepped(layer, total, peak):
    new = [None] * len(layer)
    for block in (3, 1, 2, 0):
        new[block] = layer[block] - total[block] / peak
        peak, new[block] = lax.optimization_barrier((peak, new[block]))
    return tuple(new)


def doublings(axis):
    return [(axis, 1 << k) for k in range(lax.axis_size(axis).bit_length() - 1)]


def new_probe(sums, beam):
    tile = doublings("tile")
    cuts, rest = (doublings("slab") + tile[1:], tile[:1])
    value = sums
    mine = beam
    for axis, step in cuts:
        upper = (lax.axis_index(axis) & step) != 0
        half = value.shape[1] // 2
        first, last = (value[:, :half], value[:, half:])
        got = swapped(jnp.where(upper, first, last), axis, step)
        value = jnp.where(upper, last, first) + got
        mine = jnp.where(upper, mine[:, half:], mine[:, :half])
    for axis, step in rest:
        value = value + swapped(value, axis, step)
    mine = mine - value[:2] / (value[2] + 1.0)
    for axis, step in cuts[::-1]:
        upper = (lax.axis_index(axis) & step) != 0
        got = swapped(mine, axis, step)
        mine = jnp.concatenate([jnp.where(upper, got, mine), jnp.where(upper, mine, got)], axis=1)
    return mine


def update(object_field, probe, kernel_phase, measured, positions, batch):
    side = probe.shape[-1]
    tile_rows, tile_cols = object_field.shape[2:]
    slots = positions.shape[0]
    tables = dft_tables(side)
    spans = own_spans(side, tile_rows, tile_cols) + halo_spans(side, tile_rows, tile_cols)
    places_out = grad_spans(side, tile_rows, tile_cols)
    corner = jnp.stack([lax.axis_index("tile") * tile_rows, lax.axis_index("slab") * tile_cols])
    local_at = positions - corner[None, :]
    frames = f32(slots, 2, side, side)
    grad_shapes = [f32(2, 2, rows, cols) for _, _, rows, cols in places_out]
    whole = pltpu.VMEM((2, tile_rows + side, tile_cols + side), jnp.float32)
    plane = pltpu.VMEM((2, side, side), jnp.float32)
    sems = pltpu.SemaphoreType.DMA((len(spans),))
    smem2 = [spec(SMEM)] * 2
    out_sems = pltpu.SemaphoreType.DMA((len(places_out),))
    cost = pl.CostEstimate(flops=int(slots * 40e9), bytes_accessed=16 << 20, transcendentals=0)
    params = pltpu.CompilerParams(vmem_limit_bytes=48 << 20)

    def call(body, given, number, ins, outs, out_shapes, scratch):
        def run(*refs):
            body(*given, side, slots, number, *refs)

        return pl.pallas_call(
            run,
            in_specs=ins,
            out_specs=outs,
            out_shape=out_shapes,
            scratch_shapes=scratch,
            cost_estimate=cost,
            compiler_params=params,
        )

    amplitude, phase = call(
        sort_kernel, (), 0, [spec(VMEM)] * 2, [spec(VMEM)] * 2, [f32(slots, side, side), f32(2, side, side)], []
    )(measured, kernel_phase)
    layers = [quarters(object_field[:, layer], side) for layer in range(2)]
    beam = probe
    for number in range(BATCHES):
        around = [surroundings(layers[k]) for k in range(2)]
        owns = [[object_field] if number == 0 else list(layer) for layer in layers]
        fields = [own + halo for own, halo in zip(owns, around)]
        counts = [len(field) for field in fields]
        patches, incoming = call(
            first_kernel,
            (spans,),
            number,
            smem2 + [spec(VMEM)] * 6 + [spec(ANY)] * counts[0],
            [spec(VMEM)] * 2,
            [frames, frames],
            [whole, plane, sems],
        )(local_at, batch, beam, phase, *tables, *fields[0])
        sums, *grads = call(
            second_kernel,
            (spans,),
            number,
            smem2 + [spec(VMEM)] * 9 + [spec(ANY)] * counts[1],
            [spec(VMEM)] + [spec(ANY)] * len(grad_shapes),
            [f32(3, side, side)] + grad_shapes,
            [whole, whole, whole, plane, plane, pltpu.VMEM(frames.shape, jnp.float32), plane, sems, out_sems],
        )(local_at, batch, beam, phase, patches, incoming, amplitude, *tables, *fields[1])
        peak = jnp.max(beam[0] * beam[0] + beam[1] * beam[1])
        total = gathered(grads)
        layers = [stepped(layers[k], total[k], peak) for k in range(2)]
        beam = new_probe(sums, beam)
    result = jnp.zeros((2, 2 * tile_rows, tile_cols), jnp.float32)
    for block in (3, 1, 2, 0):
        for layer in (0, 1):
            row, col, _, _ = spans[block]
            result = lax.dynamic_update_slice(result, layers[layer][block], (0, layer * tile_rows + row, col))
    result = result.reshape(object_field.shape)
    return (result, beam)


def solution(mesh):
    in_specs = (
        P(None, None, "tile", "slab"),
        P(),
        P(),
        P(("tile", "slab"), None, None),
        P(("tile", "slab"), None),
        P(("tile", "slab")),
    )
    out_specs = (P(None, None, "tile", "slab"), P())
    return jax.shard_map(update, mesh=mesh, in_specs=in_specs, out_specs=out_specs, check_vma=False)
```

profile of v0, /device:TPU:0, one launch (start us, length us, event | category | flops | bytes accessed | tf_op | source)
XLA Modules:
  0.0 378.4 jit_solution(16995809355815608360)
XLA Ops:
  12.7 10.2 %collective-permute-done.2.refs_11_ = f32[2,256,256]{2,1,0:T(8,128)} collective-permute-done((f32[2,256,256]{2,1,0:T(8,128)}, f32[2,256,256]{2,1,0:T(8,128)}, u32[]{:S(2)}, u32[]{:S(2)}) %collective-permute-start.2) | collective-permute-done | bytes 524320 | tf_op jit(solution)/shard_map/ppermute | solution.py:19
  24.3 4.2 %shard_map.113 = (f32[4,256,256]{2,1,0:T(8,128)S(1)}, f32[2,256,256]{2,1,0:T(8,128)S(1)}) custom-call(f32[4,256,256]{2,1,0:T(8,128)S(1)} %copy-done.5, f32[256,256]{1,0:T(8,128)S(1)} %copy-done.6), custom_call_target="tpu_custom_call" | custom-call | flops 160000000000 | bytes 16777216 | tf_op jit(solution)/shard_map/pallas_call | solution.py:558
  29.6 4.5 %collective-permute-done.7.refs_14_ = f32[2,256,256]{2,1,0:T(8,128)} collective-permute-done((f32[2,256,256]{2,1,0:T(8,128)}, f32[2,256,256]{2,1,0:T(8,128)}, u32[]{:S(2)}, u32[]{:S(2)}) %collective-permute-start.7) | collective-permute-done | bytes 524320 | tf_op jit(solution)/shard_map/ppermute | solution.py:19
  35.4 9.1 %collective-permute-done.3.refs_12_ = f32[2,256,256]{2,1,0:T(8,128)} collective-permute-done((f32[2,256,256]{2,1,0:T(8,128)}, f32[2,256,256]{2,1,0:T(8,128)}, u32[]{:S(2)}, u32[]{:S(2)}) %collective-permute-start.3) | collective-permute-done | bytes 524320 | tf_op jit(solution)/shard_map/ppermute | solution.py:19
  48.5 9.7 %shard_map.114 = (f32[4,2,256,256]{3,2,1,0:T(8,128)}, f32[4,2,256,256]{3,2,1,0:T(8,128)}) custom-call(s32[4,2]{1,0:T(4,128)S(1)} %broadcast_subtract_fusion.refs_0_, s32[4]{0:T(128)S(1)} %copy-done.7, f32[2,256,256]{2,1,0:T(8,128)S(1)} %copy-done.2, f32[2,256,256]{2,1,0:T(8,128)S(1)} %get-tuple-element.54.refs_3_, bf16[2,512,256]{2,1,0:T(8,128)(2,1)S(1)} %copy-done.9, ...), custom_call_target="tpu_custom_call" | custom-call | flops 160000000000 | bytes 16777216 | tf_op jit(solution)/shard_map/pallas_call | solution.py:568
  60.4 18.6 %shard_map.115 = (f32[3,256,256]{2,1,0:T(8,128)S(1)}, f32[2,2,256,256]{3,2,1,0:T(8,128)}, f32[2,2,256,256]{3,2,1,0:T(8,128)}, f32[2,2,256,256]{3,2,1,0:T(8,128)}...) custom-call(s32[4,2]{1,0:T(4,128)S(1)} %broadcast_subtract_fusion.re, ...), custom_call_target="tpu_custom_call" | custom-call | flops 160000000000 | bytes 16777216 | tf_op jit(solution)/shard_map/pallas_call | solution.py:577
  79.1 15.6 %collective-permute-start.10 = (f32[3,128,256]{2,1,0:T(8,128)S(1)}, f32[3,128,256]{2,1,0:T(8,128)}, u32[]{:S(2)}, u32[]{:S(2)}) collective-permute-start(f32[3,128,256]{2,1,0:T(8,128)S(1)} %slice_select_fusion.1), channel_id=1, source_target_pairs={{0,1},{1,0},{2,3},{3,2},{4,5},{5,4},{6,7},{7,6},{8,9},{9,8},{10,11... | collective-permute-start | bytes 1179656 | tf_op jit(solution)/shard_map/ppermute | solution.py:24
  97.4 7.2 %collective-permute-done.11 = f32[3,64,256]{2,1,0:T(8,128)S(1)} collective-permute-done((f32[3,64,256]{2,1,0:T(8,128)S(1)}, f32[3,64,256]{2,1,0:T(8,128)S(1)}, u32[]{:S(2)}, u32[]{:S(2)}) %collective-permute-start.11) | collective-permute-done | bytes 196640 | tf_op jit(solution)/shard_map/ppermute | solution.py:24
  106.0 4.2 %collective-permute-done.12 = f32[3,32,256]{2,1,0:T(8,128)} collective-permute-done((f32[3,32,256]{2,1,0:T(8,128)}, f32[3,32,256]{2,1,0:T(8,128)}, u32[]{:S(2)}, u32[]{:S(2)}) %collective-permute-start.12) | collective-permute-done | bytes 98336 | tf_op jit(solution)/shard_map/ppermute | solution.py:24
  112.2 4.0 %collective-permute-done.13 = f32[3,16,256]{2,1,0:T(8,128)S(1)} collective-permute-done((f32[3,16,256]{2,1,0:T(8,128)S(1)}, f32[3,16,256]{2,1,0:T(8,128)S(1)}, u32[]{:S(2)}, u32[]{:S(2)}) %collective-permute-start.13) | collective-permute-done | bytes 49184 | tf_op jit(solution)/shard_map/ppermute | solution.py:24
  116.2 3.4 collective-permute-start.14
  120.9 3.0 collective-permute-start.20
  133.7 22.5 %collective-permute-start.28 = (f32[2,256,256]{2,1,0:T(8,128)S(1)}, f32[2,256,256]{2,1,0:T(8,128)S(1)}, u32[]{:S(2)}, u32[]{:S(2)}) collective-permute-start(f32[2,256,256]{2,1,0:T(8,128)S(1)} %get-tuple-element.123), channel_id=1, source_target_pairs={{0,4},{4,8},{8,12},{12,16},{16,20},{20,24},{24,28},{1,5},{5,9},{9,... | collective-permute-start | bytes 1572872 | tf_op jit(solution)/shard_map/ppermute | solution.py:19
  161.8 6.7 %collective-permute-done.28 = f32[2,256,256]{2,1,0:T(8,128)S(1)} collective-permute-done((f32[2,256,256]{2,1,0:T(8,128)S(1)}, f32[2,256,256]{2,1,0:T(8,128)S(1)}, u32[]{:S(2)}, u32[]{:S(2)}) %collective-permute-start.28) | collective-permute-done | bytes 524320 | tf_op jit(solution)/shard_map/ppermute | solution.py:19
  168.5 9.0 %collective-permute-done.22 = f32[2,256,256]{2,1,0:T(8,128)S(1)} collective-permute-done((f32[2,256,256]{2,1,0:T(8,128)S(1)}, f32[2,256,256]{2,1,0:T(8,128)S(1)}, u32[]{:S(2)}, u32[]{:S(2)}) %collective-permute-start.22) | collective-permute-done | bytes 524320 | tf_op jit(solution)/shard_map/ppermute | solution.py:19
  186.0 10.5 %collective-permute-done.25.refs_14_ = f32[2,256,256]{2,1,0:T(8,128)S(1)} collective-permute-done((f32[2,256,256]{2,1,0:T(8,128)S(1)}, f32[2,256,256]{2,1,0:T(8,128)S(1)}, u32[]{:S(2)}, u32[]{:S(2)}) %collective-permute-start.25) | collective-permute-done | bytes 524320 | tf_op jit(solution)/shard_map/ppermute | solution.py:19
  198.7 9.0 %collective-permute-done.26.refs_15_ = f32[2,256,256]{2,1,0:T(8,128)S(1)} collective-permute-done((f32[2,256,256]{2,1,0:T(8,128)S(1)}, f32[2,256,256]{2,1,0:T(8,128)S(1)}, u32[]{:S(2)}, u32[]{:S(2)}) %collective-permute-start.26) | collective-permute-done | bytes 524320 | tf_op jit(solution)/shard_map/ppermute | solution.py:19
  210.3 8.7 %collective-permute-done.31.refs_17_ = f32[2,256,256]{2,1,0:T(8,128)} collective-permute-done((f32[2,256,256]{2,1,0:T(8,128)}, f32[2,256,256]{2,1,0:T(8,128)}, u32[]{:S(2)}, u32[]{:S(2)}) %collective-permute-start.31) | collective-permute-done | bytes 524320 | tf_op jit(solution)/shard_map/ppermute | solution.py:19
  222.5 8.8 %shard_map.116 = (f32[4,2,256,256]{3,2,1,0:T(8,128)}, f32[4,2,256,256]{3,2,1,0:T(8,128)}) custom-call(s32[4,2]{1,0:T(4,128)S(1)} %broadcast_subtract_fusion.refs_0_, s32[4]{0:T(128)S(1)} %copy-done.7, f32[2,256,256]{2,1,0:T(8,128)S(1)} %pad_maximum_fusion.refs_2_, f32[2,256,256]{2,1,0:T(8,128)S(1)} %get-tuple-element.54.refs_3_, ...), custom_call_target="tpu_custom_call" | custom-call | flops 160000000000 | bytes 16777216 | tf_op jit(solution)/shard_map/pallas_call | solution.py:568
  231.3 19.3 %shard_map.117 = (f32[3,256,256]{2,1,0:T(8,128)}, f32[2,2,256,256]{3,2,1,0:T(8,128)}, f32[2,2,256,256]{3,2,1,0:T(8,128)}, f32[2,2,256,256]{3,2,1,0:T(8,128)}, f3...) custom-call(s32[4,2]{1,0:T(4,128)S(1)} %broadcast_subtract_fusion.re, ...), custom_call_target="tpu_custom_call" | custom-call | flops 160000000000 | bytes 16777216 | tf_op jit(solution)/shard_map/pallas_call | solution.py:577
  255.0 19.4 %collective-permute-start.40 = (f32[3,64,256]{2,1,0:T(8,128)S(1)}, f32[3,64,256]{2,1,0:T(8,128)S(1)}, u32[]{:S(2)}, u32[]{:S(2)}) collective-permute-start(f32[3,64,256]{2,1,0:T(8,128)S(1)} %slice_select_fusion.3), channel_id=1, source_target_pairs={{0,2},{1,3},{2,0},{3,1},{4,6},{5,7},{6,4},{7,5},{8,10},{9,11},{10,... | collective-permute-start | bytes 589832 | tf_op jit(solution)/shard_map/ppermute | solution.py:24
  274.5 5.2 %collective-permute-done.40 = f32[3,64,256]{2,1,0:T(8,128)S(1)} collective-permute-done((f32[3,64,256]{2,1,0:T(8,128)S(1)}, f32[3,64,256]{2,1,0:T(8,128)S(1)}, u32[]{:S(2)}, u32[]{:S(2)}) %collective-permute-start.40) | collective-permute-done | bytes 196640 | tf_op jit(solution)/shard_map/ppermute | solution.py:24
  279.8 4.6 %collective-permute-done.41 = f32[3,32,256]{2,1,0:T(8,128)S(1)} collective-permute-done((f32[3,32,256]{2,1,0:T(8,128)S(1)}, f32[3,32,256]{2,1,0:T(8,128)S(1)}, u32[]{:S(2)}, u32[]{:S(2)}) %collective-permute-start.41) | collective-permute-done | bytes 98336 | tf_op jit(solution)/shard_map/ppermute | solution.py:24
  284.5 4.3 %collective-permute-start.42 = (f32[3,16,256]{2,1,0:T(8,128)S(1)}, f32[3,16,256]{2,1,0:T(8,128)S(1)}, u32[]{:S(2)}, u32[]{:S(2)}) collective-permute-start(f32[3,16,256]{2,1,0:T(8,128)S(1)} %slice_select_fusion.11), channel_id=1, source_target_pairs={{0,16},{4,20},{8,24},{12,28},{16,0},{20,4},{24,8},{28,12},{1,17},{... | collective-permute-start | bytes 147464 | tf_op jit(solution)/shard_map/ppermute | solution.py:24
  301.3 4.0 %collective-permute-start.34 = (f32[2,2,256,256]{3,2,1,0:T(8,128)S(1)}, f32[2,2,256,256]{3,2,1,0:T(8,128)S(1)}, u32[]{:S(2)}, u32[]{:S(2)}) collective-permute-start(f32[2,2,256,256]{3,2,1,0:T(8,128)S(1)} %copy-done.36), channel_id=1, source_target_pairs={{0,4},{4,8},{8,12},{12,16},{16,20},{20,24},{24,28},{1,5},{5,9},{9,... | collective-permute-start | bytes 3145736 | tf_op jit(solution)/shard_map/ppermute | solution.py:19
  306.7 4.3 %collective-permute-start.35 = (f32[2,2,512,256]{3,2,1,0:T(8,128)S(1)}, f32[2,2,512,256]{3,2,1,0:T(8,128)S(1)}, u32[]{:S(2)}, u32[]{:S(2)}) collective-permute-start(f32[2,2,512,256]{3,2,1,0:T(8,128)S(1)} %copy-done.34), channel_id=1, source_target_pairs={{0,1},{1,2},{2,3},{4,5},{5,6},{6,7},{8,9},{9,10},{10,11},{12,13},{... | collective-permute-start | bytes 6291464 | tf_op jit(solution)/shard_map/ppermute | solution.py:19
  312.5 3.8 %collective-permute-done.46 = f32[2,64,256]{2,1,0:T(8,128)S(1)} collective-permute-done((f32[2,64,256]{2,1,0:T(8,128)S(1)}, f32[2,64,256]{2,1,0:T(8,128)S(1)}, u32[]{:S(2)}, u32[]{:S(2)}) %collective-permute-start.46) | collective-permute-done | bytes 131104 | tf_op jit(solution)/shard_map/ppermute | solution.py:24
  316.4 29.6 %collective-permute-start.47 = (f32[2,128,256]{2,1,0:T(8,128)S(1)}, f32[2,128,256]{2,1,0:T(8,128)S(1)}, u32[]{:S(2)}, u32[]{:S(2)}) collective-permute-start(f32[2,128,256]{2,1,0:T(8,128)S(1)} %pad_maximum_fusion.3), channel_id=1, source_target_pairs={{0,1},{1,0},{2,3},{3,2},{4,5},{5,4},{6,7},{7,6},{8,9},{9,8},{10,11... | collective-permute-start | bytes 786440 | tf_op jit(solution)/shard_map/ppermute | solution.py:24
  348.2 3.3 collective-permute-start.38
  351.6 4.1 %collective-permute-start.37 = (f32[2,256,256]{2,1,0:T(8,128)S(1)}, f32[2,256,256]{2,1,0:T(8,128)S(1)}, u32[]{:S(2)}, u32[]{:S(2)}) collective-permute-start(f32[2,256,256]{2,1,0:T(8,128)S(1)} %get-tuple-element.120), channel_id=1, source_target_pairs={{0,4},{4,8},{8,12},{12,16},{16,20},{20,24},{24,28},{1,5},{5,9},{9,... | collective-permute-start | bytes 1572872 | tf_op jit(solution)/shard_map/ppermute | solution.py:19
  358.7 5.1 %collective-permute-done.38 = f32[2,256,256]{2,1,0:T(8,128)S(1)} collective-permute-done((f32[2,256,256]{2,1,0:T(8,128)S(1)}, f32[2,256,256]{2,1,0:T(8,128)S(1)}, u32[]{:S(2)}, u32[]{:S(2)}) %collective-permute-start.38) | collective-permute-done | bytes 524320 | tf_op jit(solution)/shard_map/ppermute | solution.py:19
  363.8 10.3 %collective-permute-done.37 = f32[2,256,256]{2,1,0:T(8,128)S(1)} collective-permute-done((f32[2,256,256]{2,1,0:T(8,128)S(1)}, f32[2,256,256]{2,1,0:T(8,128)S(1)}, u32[]{:S(2)}, u32[]{:S(2)}) %collective-permute-start.37) | collective-permute-done | bytes 524320 | tf_op jit(solution)/shard_map/ppermute | solution.py:19
  (215 shorter events, 90.5 us)
Async XLA Ops:
  4.7 18.2 %collective-permute-start.2 = (f32[2,256,256]{2,1,0:T(8,128)}, f32[2,256,256]{2,1,0:T(8,128)}, u32[]{:S(2)}, u32[]{:S(2)}) collective-permute-start(f32[2,256,256]{2,1,0:T(8,128)} %get-tuple-element.132), channel_id=1, source_target_pairs={{4,0},{8,4},{12,8},{16,12},{20,16},{24,20},{28,24},{5,1},{9,5},{13... | collective-permute-start | bytes 1572872 | tf_op jit(solution)/shard_map/ppermute | solution.py:19
  6.2 40.9 %collective-permute-start = (f32[2,256,256]{2,1,0:T(8,128)}, f32[2,256,256]{2,1,0:T(8,128)}, u32[]{:S(2)}, u32[]{:S(2)}) collective-permute-start(f32[2,256,256]{2,1,0:T(8,128)} %get-tuple-element.132), channel_id=1, source_target_pairs={{1,0},{2,1},{3,2},{5,4},{6,5},{7,6},{9,8},{10,9},{11,10},{13,12},{... | collective-permute-start | bytes 1572872 | tf_op jit(solution)/shard_map/ppermute | solution.py:19
  8.8 25.3 %collective-permute-start.7 = (f32[2,256,256]{2,1,0:T(8,128)}, f32[2,256,256]{2,1,0:T(8,128)}, u32[]{:S(2)}, u32[]{:S(2)}) collective-permute-start(f32[2,256,256]{2,1,0:T(8,128)} %get-tuple-element.129), channel_id=1, source_target_pairs={{4,0},{8,4},{12,8},{16,12},{20,16},{24,20},{28,24},{5,1},{9,5},{13... | collective-permute-start | bytes 1572872 | tf_op jit(solution)/shard_map/ppermute | solution.py:19
  10.1 34.4 %collective-permute-start.3 = (f32[2,256,256]{2,1,0:T(8,128)}, f32[2,256,256]{2,1,0:T(8,128)}, u32[]{:S(2)}, u32[]{:S(2)}) collective-permute-start(f32[2,256,256]{2,1,0:T(8,128)} %get-tuple-element.130), channel_id=1, source_target_pairs={{4,0},{8,4},{12,8},{16,12},{20,16},{24,20},{28,24},{5,1},{9,5},{13... | collective-permute-start | bytes 1572872 | tf_op jit(solution)/shard_map/ppermute | solution.py:19
  11.4 34.4 %collective-permute-start.1 = (f32[2,256,256]{2,1,0:T(8,128)}, f32[2,256,256]{2,1,0:T(8,128)}, u32[]{:S(2)}, u32[]{:S(2)}) collective-permute-start(f32[2,256,256]{2,1,0:T(8,128)} %get-tuple-element.131), channel_id=1, source_target_pairs={{1,0},{2,1},{3,2},{5,4},{6,5},{7,6},{9,8},{10,9},{11,10},{13,12},{... | collective-permute-start | bytes 1572872 | tf_op jit(solution)/shard_map/ppermute | solution.py:19
  22.9 25.5 %collective-permute-start.4 = (f32[2,256,256]{2,1,0:T(8,128)}, f32[2,256,256]{2,1,0:T(8,128)}, u32[]{:S(2)}, u32[]{:S(2)}) collective-permute-start(f32[2,256,256]{2,1,0:T(8,128)} %collective-permute-done.2.refs_11_), channel_id=1, source_target_pairs={{1,0},{2,1},{3,2},{5,4},{6,5},{7,6},{9,8},{10,9},{11,10},{13,12},{... | collective-permute-start | bytes 1572872 | tf_op jit(solution)/shard_map/ppermute | solution.py:19
  34.1 26.3 %collective-permute-start.5 = (f32[2,256,256]{2,1,0:T(8,128)}, f32[2,256,256]{2,1,0:T(8,128)}, u32[]{:S(2)}, u32[]{:S(2)}) collective-permute-start(f32[2,256,256]{2,1,0:T(8,128)} %get-tuple-element.129), channel_id=1, source_target_pairs={{1,0},{2,1},{3,2},{5,4},{6,5},{7,6},{9,8},{10,9},{11,10},{13,12},{... | collective-permute-start | bytes 1572872 | tf_op jit(solution)/shard_map/ppermute | solution.py:19
  44.5 15.9 %collective-permute-start.8 = (f32[2,256,256]{2,1,0:T(8,128)}, f32[2,256,256]{2,1,0:T(8,128)}, u32[]{:S(2)}, u32[]{:S(2)}) collective-permute-start(f32[2,256,256]{2,1,0:T(8,128)} %get-tuple-element.127), channel_id=1, source_target_pairs={{4,0},{8,4},{12,8},{16,12},{20,16},{24,20},{28,24},{5,1},{9,5},{13... | collective-permute-start | bytes 1572872 | tf_op jit(solution)/shard_map/ppermute | solution.py:19
  45.8 14.6 %collective-permute-start.6 = (f32[2,256,256]{2,1,0:T(8,128)}, f32[2,256,256]{2,1,0:T(8,128)}, u32[]{:S(2)}, u32[]{:S(2)}) collective-permute-start(f32[2,256,256]{2,1,0:T(8,128)} %get-tuple-element.128), channel_id=1, source_target_pairs={{1,0},{2,1},{3,2},{5,4},{6,5},{7,6},{9,8},{10,9},{11,10},{13,12},{... | collective-permute-start | bytes 1572872 | tf_op jit(solution)/shard_map/ppermute | solution.py:19
  47.1 13.3 %collective-permute-start.9 = (f32[2,256,256]{2,1,0:T(8,128)}, f32[2,256,256]{2,1,0:T(8,128)}, u32[]{:S(2)}, u32[]{:S(2)}) collective-permute-start(f32[2,256,256]{2,1,0:T(8,128)} %collective-permute-done.7.refs_14_), channel_id=1, source_target_pairs={{1,0},{2,1},{3,2},{5,4},{6,5},{7,6},{9,8},{10,9},{11,10},{13,12},{... | collective-permute-start | bytes 1572872 | tf_op jit(solution)/shard_map/ppermute | solution.py:19
  79.1 17.1 %collective-permute-start.10 = (f32[3,128,256]{2,1,0:T(8,128)S(1)}, f32[3,128,256]{2,1,0:T(8,128)}, u32[]{:S(2)}, u32[]{:S(2)}) collective-permute-start(f32[3,128,256]{2,1,0:T(8,128)S(1)} %slice_select_fusion.1), channel_id=1, source_target_pairs={{0,1},{1,0},{2,3},{3,2},{4,5},{5,4},{6,7},{7,6},{8,9},{9,8},{10,11... | collective-permute-start | bytes 1179656 | tf_op jit(solution)/shard_map/ppermute | solution.py:24
  119.6 14.0 %collective-permute-start.21 = (f32[2,2,256,256]{3,2,1,0:T(8,128)}, f32[2,2,256,256]{3,2,1,0:T(8,128)S(1)}, u32[]{:S(2)}, u32[]{:S(2)}) collective-permute-start(f32[2,2,256,256]{3,2,1,0:T(8,128)} %get-tuple-element.70), channel_id=1, source_target_pairs={{0,1},{1,2},{2,3},{4,5},{5,6},{6,7},{8,9},{9,10},{10,11},{12,13},{... | collective-permute-start | bytes 3145736 | tf_op jit(solution)/shard_map/ppermute | solution.py:19
  120.9 39.1 %collective-permute-start.20 = (f32[2,2,512,256]{3,2,1,0:T(8,128)}, f32[2,2,512,256]{3,2,1,0:T(8,128)S(1)}, u32[]{:S(2)}, u32[]{:S(2)}) collective-permute-start(f32[2,2,512,256]{3,2,1,0:T(8,128)} %get-tuple-element.66), channel_id=1, source_target_pairs={{0,1},{1,2},{2,3},{4,5},{5,6},{6,7},{8,9},{9,10},{10,11},{12,13},{... | collective-permute-start | bytes 6291464 | tf_op jit(solution)/shard_map/ppermute | solution.py:19
  124.8 33.4 %collective-permute-start.19 = (f32[2,2,256,256]{3,2,1,0:T(8,128)}, f32[2,2,256,256]{3,2,1,0:T(8,128)S(1)}, u32[]{:S(2)}, u32[]{:S(2)}) collective-permute-start(f32[2,2,256,256]{3,2,1,0:T(8,128)} %get-tuple-element.63), channel_id=1, source_target_pairs={{0,4},{4,8},{8,12},{12,16},{16,20},{20,24},{24,28},{1,5},{5,9},{9,... | collective-permute-start | bytes 3145736 | tf_op jit(solution)/shard_map/ppermute | solution.py:19
  133.5 47.1 %collective-permute-start.17 = (f32[2,64,256]{2,1,0:T(8,128)S(1)}, f32[2,64,256]{2,1,0:T(8,128)S(1)}, u32[]{:S(2)}, u32[]{:S(2)}) collective-permute-start(f32[2,64,256]{2,1,0:T(8,128)S(1)} %pad_maximum_fusion.4), channel_id=1, source_target_pairs={{0,2},{1,3},{2,0},{3,1},{4,6},{5,7},{6,4},{7,5},{8,10},{9,11},{10,... | collective-permute-start | bytes 393224 | tf_op jit(solution)/shard_map/ppermute | solution.py:24
  133.7 34.7 %collective-permute-start.28 = (f32[2,256,256]{2,1,0:T(8,128)S(1)}, f32[2,256,256]{2,1,0:T(8,128)S(1)}, u32[]{:S(2)}, u32[]{:S(2)}) collective-permute-start(f32[2,256,256]{2,1,0:T(8,128)S(1)} %get-tuple-element.123), channel_id=1, source_target_pairs={{0,4},{4,8},{8,12},{12,16},{16,20},{20,24},{24,28},{1,5},{5,9},{9,... | collective-permute-start | bytes 1572872 | tf_op jit(solution)/shard_map/ppermute | solution.py:19
  156.2 21.3 %collective-permute-start.22 = (f32[2,256,256]{2,1,0:T(8,128)S(1)}, f32[2,256,256]{2,1,0:T(8,128)S(1)}, u32[]{:S(2)}, u32[]{:S(2)}) collective-permute-start(f32[2,256,256]{2,1,0:T(8,128)S(1)} %get-tuple-element.124), channel_id=1, source_target_pairs={{0,4},{4,8},{8,12},{12,16},{16,20},{20,24},{24,28},{1,5},{5,9},{9,... | collective-permute-start | bytes 1572872 | tf_op jit(solution)/shard_map/ppermute | solution.py:19
  179.3 17.1 %collective-permute-start.25 = (f32[2,256,256]{2,1,0:T(8,128)S(1)}, f32[2,256,256]{2,1,0:T(8,128)S(1)}, u32[]{:S(2)}, u32[]{:S(2)}) collective-permute-start(f32[2,256,256]{2,1,0:T(8,128)S(1)} %get-tuple-element.71.refs_8_), channel_id=1, source_target_pairs={{4,0},{8,4},{12,8},{16,12},{20,16},{24,20},{28,24},{5,1},{9,5},{13... | collective-permute-start | bytes 1572872 | tf_op jit(solution)/shard_map/ppermute | solution.py:19
  180.7 26.9 %collective-permute-start.26 = (f32[2,256,256]{2,1,0:T(8,128)S(1)}, f32[2,256,256]{2,1,0:T(8,128)S(1)}, u32[]{:S(2)}, u32[]{:S(2)}) collective-permute-start(f32[2,256,256]{2,1,0:T(8,128)S(1)} %get-tuple-element.72.refs_9_), channel_id=1, source_target_pairs={{4,0},{8,4},{12,8},{16,12},{20,16},{24,20},{28,24},{5,1},{9,5},{13... | collective-permute-start | bytes 1572872 | tf_op jit(solution)/shard_map/ppermute | solution.py:19
  182.0 26.9 %collective-permute-start.23 = (f32[2,256,256]{2,1,0:T(8,128)S(1)}, f32[2,256,256]{2,1,0:T(8,128)S(1)}, u32[]{:S(2)}, u32[]{:S(2)}) collective-permute-start(f32[2,256,256]{2,1,0:T(8,128)S(1)} %get-tuple-element.71.refs_8_), channel_id=1, source_target_pairs={{1,0},{2,1},{3,2},{5,4},{6,5},{7,6},{9,8},{10,9},{11,10},{13,12},{... | collective-permute-start | bytes 1572872 | tf_op jit(solution)/shard_map/ppermute | solution.py:19
  183.3 35.7 %collective-permute-start.31 = (f32[2,256,256]{2,1,0:T(8,128)}, f32[2,256,256]{2,1,0:T(8,128)}, u32[]{:S(2)}, u32[]{:S(2)}) collective-permute-start(f32[2,256,256]{2,1,0:T(8,128)} %get-tuple-element.79.refs_11_), channel_id=1, source_target_pairs={{4,0},{8,4},{12,8},{16,12},{20,16},{24,20},{28,24},{5,1},{9,5},{13... | collective-permute-start | bytes 1572872 | tf_op jit(solution)/shard_map/ppermute | solution.py:19
  184.7 35.7 %collective-permute-start.24 = (f32[2,256,256]{2,1,0:T(8,128)S(1)}, f32[2,256,256]{2,1,0:T(8,128)S(1)}, u32[]{:S(2)}, u32[]{:S(2)}) collective-permute-start(f32[2,256,256]{2,1,0:T(8,128)S(1)} %get-tuple-element.73.refs_10_), channel_id=1, source_target_pairs={{1,0},{2,1},{3,2},{5,4},{6,5},{7,6},{9,8},{10,9},{11,10},{13,12},{... | collective-permute-start | bytes 1572872 | tf_op jit(solution)/shard_map/ppermute | solution.py:19
  196.5 25.2 %collective-permute-start.27 = (f32[2,256,256]{2,1,0:T(8,128)S(1)}, f32[2,256,256]{2,1,0:T(8,128)S(1)}, u32[]{:S(2)}, u32[]{:S(2)}) collective-permute-start(f32[2,256,256]{2,1,0:T(8,128)S(1)} %collective-permute-done.25.refs_14_), channel_id=1, source_target_pairs={{1,0},{2,1},{3,2},{5,4},{6,5},{7,6},{9,8},{10,9},{11,10},{13,12},{... | collective-permute-start | bytes 1572872 | tf_op jit(solution)/shard_map/ppermute | solution.py:19
  207.7 23.6 %collective-permute-start.32 = (f32[2,256,256]{2,1,0:T(8,128)}, f32[2,256,256]{2,1,0:T(8,128)}, u32[]{:S(2)}, u32[]{:S(2)}) collective-permute-start(f32[2,256,256]{2,1,0:T(8,128)} %get-tuple-element.80.refs_12_), channel_id=1, source_target_pairs={{4,0},{8,4},{12,8},{16,12},{20,16},{24,20},{28,24},{5,1},{9,5},{13... | collective-permute-start | bytes 1572872 | tf_op jit(solution)/shard_map/ppermute | solution.py:19
  209.0 22.3 %collective-permute-start.29 = (f32[2,256,256]{2,1,0:T(8,128)}, f32[2,256,256]{2,1,0:T(8,128)}, u32[]{:S(2)}, u32[]{:S(2)}) collective-permute-start(f32[2,256,256]{2,1,0:T(8,128)} %get-tuple-element.79.refs_11_), channel_id=1, source_target_pairs={{1,0},{2,1},{3,2},{5,4},{6,5},{7,6},{9,8},{10,9},{11,10},{13,12},{... | collective-permute-start | bytes 1572872 | tf_op jit(solution)/shard_map/ppermute | solution.py:19
  255.0 24.6 %collective-permute-start.40 = (f32[3,64,256]{2,1,0:T(8,128)S(1)}, f32[3,64,256]{2,1,0:T(8,128)S(1)}, u32[]{:S(2)}, u32[]{:S(2)}) collective-permute-start(f32[3,64,256]{2,1,0:T(8,128)S(1)} %slice_select_fusion.3), channel_id=1, source_target_pairs={{0,2},{1,3},{2,0},{3,1},{4,6},{5,7},{6,4},{7,5},{8,10},{9,11},{10,... | collective-permute-start | bytes 589832 | tf_op jit(solution)/shard_map/ppermute | solution.py:24
  301.3 44.7 %collective-permute-start.34 = (f32[2,2,256,256]{3,2,1,0:T(8,128)S(1)}, f32[2,2,256,256]{3,2,1,0:T(8,128)S(1)}, u32[]{:S(2)}, u32[]{:S(2)}) collective-permute-start(f32[2,2,256,256]{3,2,1,0:T(8,128)S(1)} %copy-done.36), channel_id=1, source_target_pairs={{0,4},{4,8},{8,12},{12,16},{16,20},{20,24},{24,28},{1,5},{5,9},{9,... | collective-permute-start | bytes 3145736 | tf_op jit(solution)/shard_map/ppermute | solution.py:19
  305.3 42.8 %collective-permute-start.36 = (f32[2,2,256,256]{3,2,1,0:T(8,128)S(1)}, f32[2,2,256,256]{3,2,1,0:T(8,128)S(1)}, u32[]{:S(2)}, u32[]{:S(2)}) collective-permute-start(f32[2,2,256,256]{3,2,1,0:T(8,128)S(1)} %copy-done.35), channel_id=1, source_target_pairs={{0,1},{1,2},{2,3},{4,5},{5,6},{6,7},{8,9},{9,10},{10,11},{12,13},{... | collective-permute-start | bytes 3145736 | tf_op jit(solution)/shard_map/ppermute | solution.py:19
  306.7 50.0 %collective-permute-start.35 = (f32[2,2,512,256]{3,2,1,0:T(8,128)S(1)}, f32[2,2,512,256]{3,2,1,0:T(8,128)S(1)}, u32[]{:S(2)}, u32[]{:S(2)}) collective-permute-start(f32[2,2,512,256]{3,2,1,0:T(8,128)S(1)} %copy-done.34), channel_id=1, source_target_pairs={{0,1},{1,2},{2,3},{4,5},{5,6},{6,7},{8,9},{9,10},{10,11},{12,13},{... | collective-permute-start | bytes 6291464 | tf_op jit(solution)/shard_map/ppermute | solution.py:19
  316.4 39.3 %collective-permute-start.47 = (f32[2,128,256]{2,1,0:T(8,128)S(1)}, f32[2,128,256]{2,1,0:T(8,128)S(1)}, u32[]{:S(2)}, u32[]{:S(2)}) collective-permute-start(f32[2,128,256]{2,1,0:T(8,128)S(1)} %pad_maximum_fusion.3), channel_id=1, source_target_pairs={{0,1},{1,0},{2,3},{3,2},{4,5},{5,4},{6,7},{7,6},{8,9},{9,8},{10,11... | collective-permute-start | bytes 786440 | tf_op jit(solution)/shard_map/ppermute | solution.py:24
  348.2 15.6 %collective-permute-start.38 = (f32[2,256,256]{2,1,0:T(8,128)S(1)}, f32[2,256,256]{2,1,0:T(8,128)S(1)}, u32[]{:S(2)}, u32[]{:S(2)}) collective-permute-start(f32[2,256,256]{2,1,0:T(8,128)S(1)} %get-tuple-element.119), channel_id=1, source_target_pairs={{0,4},{4,8},{8,12},{12,16},{16,20},{20,24},{24,28},{1,5},{5,9},{9,... | collective-permute-start | bytes 1572872 | tf_op jit(solution)/shard_map/ppermute | solution.py:19
  351.6 22.6 %collective-permute-start.37 = (f32[2,256,256]{2,1,0:T(8,128)S(1)}, f32[2,256,256]{2,1,0:T(8,128)S(1)}, u32[]{:S(2)}, u32[]{:S(2)}) collective-permute-start(f32[2,256,256]{2,1,0:T(8,128)S(1)} %get-tuple-element.120), channel_id=1, source_target_pairs={{0,4},{4,8},{8,12},{12,16},{16,20},{20,24},{24,28},{1,5},{5,9},{9,... | collective-permute-start | bytes 1572872 | tf_op jit(solution)/shard_map/ppermute | solution.py:19
  (55 other events, 1150.8 us)
where the time goes:
time: 381 us; the launch traced here: 378 us
  starting transfers between devices  153 us (40%)
  waiting for transfers between devices  127 us (33%)
  Pallas kernels  60.6 us (16%)
  other arithmetic  24.9 us (7%)
  local copies, waits for them, and re-layouts  10.2 us (3%)
    ppermute x30, waiting for transfers between devices, shifted(): lax.ppermute(value, axis, [(source, source + steps) for source in range(f...  85.3 us
    ppermute x18, starting transfers between devices, swapped(): lax.ppermute(value, axis, [(source, source ^ step) for source in range(co...  79.4 us
    ppermute x30, starting transfers between devices, shifted(): lax.ppermute(value, axis, [(source, source + steps) for source in range(f...  74 us
    ppermute x18, waiting for transfers between devices, swapped(): lax.ppermute(value, axis, [(source, source ^ step) for source in range(co...  42.2 us
    pallas_call x2, Pallas kernels, update(): call(second_kernel, (spans,), number, smem2 + [spec(VMEM)] * 9 + [spec(AN...  37.9 us
    pallas_call x2, Pallas kernels, update(): call(first_kernel, (spans,), number, smem2 + [spec(VMEM)] * 6 + [spec(ANY...  18.5 us
    sub x8, other arithmetic, stepped(): new[block] = layer[block] - total[block] / peak  14.2 us
  transfers between devices with their start and end apart: 48, of which 24 were waited for; matrix products, arithmetic and copies ran while one was open for 5% of the time, Pallas kernels for 6%

commit v1 on v0

--- a/solution.py
+++ b/solution.py
@@ -188,11 +188,10 @@
         value = pltpu.roll(value, up, 1)
         return jnp.where(take_rows, value[:groups], value[1:])
 
-    for part in range(field.shape[0]):
-
-        @pl.loop(0, side // STRIP)
-        def _(step):
-            down = pl.multiple_of(step * STRIP, STRIP)
+    @pl.loop(0, side // STRIP)
+    def _(step):
+        down = pl.multiple_of(step * STRIP, STRIP)
+        for part in range(field.shape[0]):
             turned = [read(part, down, k) for k in range(side // LANES + 1)]
             for k in range(side // LANES):
                 value = jnp.where(take_cols, turned[k], turned[k + 1])
@@ -216,11 +215,11 @@
             keep_rows, jnp.concatenate([value, edge], axis=0), jnp.concatenate([edge, value], axis=0)
         )
 
-    for part in range(field.shape[0]):
-
-        @pl.loop(0, side // STRIP)
-        def _(step):
-            down = pl.multiple_of(step * STRIP, STRIP)
+    @pl.loop(0, side // STRIP)
+    def _(step):
+        down = pl.multiple_of(step * STRIP, STRIP)
+        writes = []
+        for part in range(field.shape[0]):
             turned = [blank] + [read(part, down, k) for k in range(count)] + [blank]
             for k in range(count + 1):
                 value = jnp.where(keep_cols, turned[k + 1], turned[k]).reshape(STRIP + ROWS, LANES)
@@ -229,7 +228,9 @@
                     pl.ds(pl.multiple_of(top + down, ROWS), STRIP + ROWS),
                     pl.ds(pl.multiple_of(left + k * LANES, LANES), LANES),
                 )
-                field[spot] = field[spot] + value
+                writes.append((spot, field[spot] + value))
+        for spot, value in writes:
+            field[spot] = value
 
 
 def halo_spans(side, rows, cols):

time: 381 us -> 372 us (0.976)
  starting transfers between devices: 153 us -> 148 us
  Pallas kernels: 60.6 us -> 55.9 us
    ppermute x18, starting transfers between devices: 79.4 us -> 74.1 us  [swapped(): lax.ppermute(value, axis, [(source, source ^ step) for source in range(co...]
where the time goes in v1:
time: 372 us; the launch traced here: 369 us
  starting transfers between devices  148 us (40%)
  waiting for transfers between devices  128 us (34%)
  Pallas kernels  55.9 us (15%)
  other arithmetic  24.9 us (7%)
  local copies, waits for them, and re-layouts  10.2 us (3%)
    ppermute x30, waiting for transfers between devices, shifted(): lax.ppermute(value, axis, [(source, source + steps) for source in range(f...  85.8 us
    ppermute x18, starting transfers between devices, swapped(): lax.ppermute(value, axis, [(source, source ^ step) for source in range(co...  74.1 us
    ppermute x30, starting transfers between devices, shifted(): lax.ppermute(value, axis, [(source, source + steps) for source in range(f...  74 us
    ppermute x18, waiting for transfers between devices, swapped(): lax.ppermute(value, axis, [(source, source ^ step) for source in range(co...  42.2 us
    pallas_call x2, Pallas kernels, update(): call(second_kernel, (spans,), number, smem2 + [spec(VMEM)] * 9 + [spec(AN...  34.3 us
    pallas_call x2, Pallas kernels, update(): call(first_kernel, (spans,), number, smem2 + [spec(VMEM)] * 6 + [spec(ANY...  17.4 us
    sub x8, other arithmetic, stepped(): new[block] = layer[block] - total[block] / peak  14.2 us
  transfers between devices with their start and end apart: 48, of which 24 were waited for; matrix products, arithmetic and copies ran while one was open for 5% of the time, Pallas kernels for 6%

profile of v1, /device:TPU:0, one launch (start us, length us, event | category | flops | bytes accessed | tf_op | source)
XLA Modules:
  0.0 369.1 jit_solution(58449599819048351)
XLA Ops:
  12.7 10.2 %collective-permute-done.2.refs_11_ = f32[2,256,256]{2,1,0:T(8,128)} collective-permute-done((f32[2,256,256]{2,1,0:T(8,128)}, f32[2,256,256]{2,1,0:T(8,128)}, u32[]{:S(2)}, u32[]{:S(2)}) %collective-permute-start.2) | collective-permute-done | bytes 524320 | tf_op jit(solution)/shard_map/ppermute | solution.py:19
  24.3 4.2 %shard_map.113 = (f32[4,256,256]{2,1,0:T(8,128)S(1)}, f32[2,256,256]{2,1,0:T(8,128)S(1)}) custom-call(f32[4,256,256]{2,1,0:T(8,128)S(1)} %copy-done.5, f32[256,256]{1,0:T(8,128)S(1)} %copy-done.6), custom_call_target="tpu_custom_call" | custom-call | flops 160000000000 | bytes 16777216 | tf_op jit(solution)/shard_map/pallas_call | solution.py:559
  29.6 4.5 %collective-permute-done.7.refs_14_ = f32[2,256,256]{2,1,0:T(8,128)} collective-permute-done((f32[2,256,256]{2,1,0:T(8,128)}, f32[2,256,256]{2,1,0:T(8,128)}, u32[]{:S(2)}, u32[]{:S(2)}) %collective-permute-start.7) | collective-permute-done | bytes 524320 | tf_op jit(solution)/shard_map/ppermute | solution.py:19
  35.4 9.1 %collective-permute-done.3.refs_12_ = f32[2,256,256]{2,1,0:T(8,128)} collective-permute-done((f32[2,256,256]{2,1,0:T(8,128)}, f32[2,256,256]{2,1,0:T(8,128)}, u32[]{:S(2)}, u32[]{:S(2)}) %collective-permute-start.3) | collective-permute-done | bytes 524320 | tf_op jit(solution)/shard_map/ppermute | solution.py:19
  48.5 9.1 %shard_map.114 = (f32[4,2,256,256]{3,2,1,0:T(8,128)}, f32[4,2,256,256]{3,2,1,0:T(8,128)}) custom-call(s32[4,2]{1,0:T(4,128)S(1)} %broadcast_subtract_fusion.refs_0_, s32[4]{0:T(128)S(1)} %copy-done.7, f32[2,256,256]{2,1,0:T(8,128)S(1)} %copy-done.2, f32[2,256,256]{2,1,0:T(8,128)S(1)} %get-tuple-element.54.refs_3_, bf16[2,512,256]{2,1,0:T(8,128)(2,1)S(1)} %copy-done.9, ...), custom_call_target="tpu_custom_call" | custom-call | flops 160000000000 | bytes 16777216 | tf_op jit(solution)/shard_map/pallas_call | solution.py:569
  60.4 16.9 %shard_map.115 = (f32[3,256,256]{2,1,0:T(8,128)S(1)}, f32[2,2,256,256]{3,2,1,0:T(8,128)}, f32[2,2,256,256]{3,2,1,0:T(8,128)}, f32[2,2,256,256]{3,2,1,0:T(8,128)}...) custom-call(s32[4,2]{1,0:T(4,128)S(1)} %broadcast_subtract_fusion.re, ...), custom_call_target="tpu_custom_call" | custom-call | flops 160000000000 | bytes 16777216 | tf_op jit(solution)/shard_map/pallas_call | solution.py:578
  77.3 12.7 %collective-permute-start.10 = (f32[3,128,256]{2,1,0:T(8,128)S(1)}, f32[3,128,256]{2,1,0:T(8,128)}, u32[]{:S(2)}, u32[]{:S(2)}) collective-permute-start(f32[3,128,256]{2,1,0:T(8,128)S(1)} %slice_select_fusion.1), channel_id=1, source_target_pairs={{0,1},{1,0},{2,3},{3,2},{4,5},{5,4},{6,7},{7,6},{8,9},{9,8},{10,11... | collective-permute-start | bytes 1179656 | tf_op jit(solution)/shard_map/ppermute | solution.py:24
  92.7 7.2 %collective-permute-done.11 = f32[3,64,256]{2,1,0:T(8,128)S(1)} collective-permute-done((f32[3,64,256]{2,1,0:T(8,128)S(1)}, f32[3,64,256]{2,1,0:T(8,128)S(1)}, u32[]{:S(2)}, u32[]{:S(2)}) %collective-permute-start.11) | collective-permute-done | bytes 196640 | tf_op jit(solution)/shard_map/ppermute | solution.py:24
  101.3 4.2 %collective-permute-done.12 = f32[3,32,256]{2,1,0:T(8,128)} collective-permute-done((f32[3,32,256]{2,1,0:T(8,128)}, f32[3,32,256]{2,1,0:T(8,128)}, u32[]{:S(2)}, u32[]{:S(2)}) %collective-permute-start.12) | collective-permute-done | bytes 98336 | tf_op jit(solution)/shard_map/ppermute | solution.py:24
  107.5 4.0 %collective-permute-done.13 = f32[3,16,256]{2,1,0:T(8,128)S(1)} collective-permute-done((f32[3,16,256]{2,1,0:T(8,128)S(1)}, f32[3,16,256]{2,1,0:T(8,128)S(1)}, u32[]{:S(2)}, u32[]{:S(2)}) %collective-permute-start.13) | collective-permute-done | bytes 49184 | tf_op jit(solution)/shard_map/ppermute | solution.py:24
  111.5 3.3 collective-permute-start.14
  116.2 3.0 collective-permute-start.20
  129.1 22.4 %collective-permute-start.28 = (f32[2,256,256]{2,1,0:T(8,128)S(1)}, f32[2,256,256]{2,1,0:T(8,128)S(1)}, u32[]{:S(2)}, u32[]{:S(2)}) collective-permute-start(f32[2,256,256]{2,1,0:T(8,128)S(1)} %get-tuple-element.123), channel_id=1, source_target_pairs={{0,4},{4,8},{8,12},{12,16},{16,20},{20,24},{24,28},{1,5},{5,9},{9,... | collective-permute-start | bytes 1572872 | tf_op jit(solution)/shard_map/ppermute | solution.py:19
  157.1 6.7 %collective-permute-done.28 = f32[2,256,256]{2,1,0:T(8,128)S(1)} collective-permute-done((f32[2,256,256]{2,1,0:T(8,128)S(1)}, f32[2,256,256]{2,1,0:T(8,128)S(1)}, u32[]{:S(2)}, u32[]{:S(2)}) %collective-permute-start.28) | collective-permute-done | bytes 524320 | tf_op jit(solution)/shard_map/ppermute | solution.py:19
  163.8 9.0 %collective-permute-done.22 = f32[2,256,256]{2,1,0:T(8,128)S(1)} collective-permute-done((f32[2,256,256]{2,1,0:T(8,128)S(1)}, f32[2,256,256]{2,1,0:T(8,128)S(1)}, u32[]{:S(2)}, u32[]{:S(2)}) %collective-permute-start.22) | collective-permute-done | bytes 524320 | tf_op jit(solution)/shard_map/ppermute | solution.py:19
  181.2 10.5 %collective-permute-done.25.refs_14_ = f32[2,256,256]{2,1,0:T(8,128)S(1)} collective-permute-done((f32[2,256,256]{2,1,0:T(8,128)S(1)}, f32[2,256,256]{2,1,0:T(8,128)S(1)}, u32[]{:S(2)}, u32[]{:S(2)}) %collective-permute-start.25) | collective-permute-done | bytes 524320 | tf_op jit(solution)/shard_map/ppermute | solution.py:19
  194.0 9.0 %collective-permute-done.26.refs_15_ = f32[2,256,256]{2,1,0:T(8,128)S(1)} collective-permute-done((f32[2,256,256]{2,1,0:T(8,128)S(1)}, f32[2,256,256]{2,1,0:T(8,128)S(1)}, u32[]{:S(2)}, u32[]{:S(2)}) %collective-permute-start.26) | collective-permute-done | bytes 524320 | tf_op jit(solution)/shard_map/ppermute | solution.py:19
  205.6 8.7 %collective-permute-done.31.refs_17_ = f32[2,256,256]{2,1,0:T(8,128)} collective-permute-done((f32[2,256,256]{2,1,0:T(8,128)}, f32[2,256,256]{2,1,0:T(8,128)}, u32[]{:S(2)}, u32[]{:S(2)}) %collective-permute-start.31) | collective-permute-done | bytes 524320 | tf_op jit(solution)/shard_map/ppermute | solution.py:19
  217.7 8.2 %shard_map.116 = (f32[4,2,256,256]{3,2,1,0:T(8,128)}, f32[4,2,256,256]{3,2,1,0:T(8,128)}) custom-call(s32[4,2]{1,0:T(4,128)S(1)} %broadcast_subtract_fusion.refs_0_, s32[4]{0:T(128)S(1)} %copy-done.7, f32[2,256,256]{2,1,0:T(8,128)S(1)} %pad_maximum_fusion.refs_2_, f32[2,256,256]{2,1,0:T(8,128)S(1)} %get-tuple-element.54.refs_3_, ...), custom_call_target="tpu_custom_call" | custom-call | flops 160000000000 | bytes 16777216 | tf_op jit(solution)/shard_map/pallas_call | solution.py:569
  226.1 17.5 %shard_map.117 = (f32[3,256,256]{2,1,0:T(8,128)}, f32[2,2,256,256]{3,2,1,0:T(8,128)}, f32[2,2,256,256]{3,2,1,0:T(8,128)}, f32[2,2,256,256]{3,2,1,0:T(8,128)}, f3...) custom-call(s32[4,2]{1,0:T(4,128)S(1)} %broadcast_subtract_fusion.re, ...), custom_call_target="tpu_custom_call" | custom-call | flops 160000000000 | bytes 16777216 | tf_op jit(solution)/shard_map/pallas_call | solution.py:578
  247.9 17.1 %collective-permute-start.40 = (f32[3,64,256]{2,1,0:T(8,128)S(1)}, f32[3,64,256]{2,1,0:T(8,128)S(1)}, u32[]{:S(2)}, u32[]{:S(2)}) collective-permute-start(f32[3,64,256]{2,1,0:T(8,128)S(1)} %slice_select_fusion.3), channel_id=1, source_target_pairs={{0,2},{1,3},{2,0},{3,1},{4,6},{5,7},{6,4},{7,5},{8,10},{9,11},{10,... | collective-permute-start | bytes 589832 | tf_op jit(solution)/shard_map/ppermute | solution.py:24
  265.1 5.2 %collective-permute-done.40 = f32[3,64,256]{2,1,0:T(8,128)S(1)} collective-permute-done((f32[3,64,256]{2,1,0:T(8,128)S(1)}, f32[3,64,256]{2,1,0:T(8,128)S(1)}, u32[]{:S(2)}, u32[]{:S(2)}) %collective-permute-start.40) | collective-permute-done | bytes 196640 | tf_op jit(solution)/shard_map/ppermute | solution.py:24
  270.4 4.6 %collective-permute-done.41 = f32[3,32,256]{2,1,0:T(8,128)S(1)} collective-permute-done((f32[3,32,256]{2,1,0:T(8,128)S(1)}, f32[3,32,256]{2,1,0:T(8,128)S(1)}, u32[]{:S(2)}, u32[]{:S(2)}) %collective-permute-start.41) | collective-permute-done | bytes 98336 | tf_op jit(solution)/shard_map/ppermute | solution.py:24
  275.1 4.3 %collective-permute-start.42 = (f32[3,16,256]{2,1,0:T(8,128)S(1)}, f32[3,16,256]{2,1,0:T(8,128)S(1)}, u32[]{:S(2)}, u32[]{:S(2)}) collective-permute-start(f32[3,16,256]{2,1,0:T(8,128)S(1)} %slice_select_fusion.11), channel_id=1, source_target_pairs={{0,16},{4,20},{8,24},{12,28},{16,0},{20,4},{24,8},{28,12},{1,17},{... | collective-permute-start | bytes 147464 | tf_op jit(solution)/shard_map/ppermute | solution.py:24
  291.9 4.0 %collective-permute-start.34 = (f32[2,2,256,256]{3,2,1,0:T(8,128)S(1)}, f32[2,2,256,256]{3,2,1,0:T(8,128)S(1)}, u32[]{:S(2)}, u32[]{:S(2)}) collective-permute-start(f32[2,2,256,256]{3,2,1,0:T(8,128)S(1)} %copy-done.36), channel_id=1, source_target_pairs={{0,4},{4,8},{8,12},{12,16},{16,20},{20,24},{24,28},{1,5},{5,9},{9,... | collective-permute-start | bytes 3145736 | tf_op jit(solution)/shard_map/ppermute | solution.py:19
  297.3 4.3 %collective-permute-start.35 = (f32[2,2,512,256]{3,2,1,0:T(8,128)S(1)}, f32[2,2,512,256]{3,2,1,0:T(8,128)S(1)}, u32[]{:S(2)}, u32[]{:S(2)}) collective-permute-start(f32[2,2,512,256]{3,2,1,0:T(8,128)S(1)} %copy-done.34), channel_id=1, source_target_pairs={{0,1},{1,2},{2,3},{4,5},{5,6},{6,7},{8,9},{9,10},{10,11},{12,13},{... | collective-permute-start | bytes 6291464 | tf_op jit(solution)/shard_map/ppermute | solution.py:19
  303.2 3.8 %collective-permute-done.46 = f32[2,64,256]{2,1,0:T(8,128)S(1)} collective-permute-done((f32[2,64,256]{2,1,0:T(8,128)S(1)}, f32[2,64,256]{2,1,0:T(8,128)S(1)}, u32[]{:S(2)}, u32[]{:S(2)}) %collective-permute-start.46) | collective-permute-done | bytes 131104 | tf_op jit(solution)/shard_map/ppermute | solution.py:24
  307.1 29.6 %collective-permute-start.47 = (f32[2,128,256]{2,1,0:T(8,128)S(1)}, f32[2,128,256]{2,1,0:T(8,128)S(1)}, u32[]{:S(2)}, u32[]{:S(2)}) collective-permute-start(f32[2,128,256]{2,1,0:T(8,128)S(1)} %pad_maximum_fusion.3), channel_id=1, source_target_pairs={{0,1},{1,0},{2,3},{3,2},{4,5},{5,4},{6,7},{7,6},{8,9},{9,8},{10,11... | collective-permute-start | bytes 786440 | tf_op jit(solution)/shard_map/ppermute | solution.py:24
  338.9 3.3 collective-permute-start.38
  342.2 4.1 %collective-permute-start.37 = (f32[2,256,256]{2,1,0:T(8,128)S(1)}, f32[2,256,256]{2,1,0:T(8,128)S(1)}, u32[]{:S(2)}, u32[]{:S(2)}) collective-permute-start(f32[2,256,256]{2,1,0:T(8,128)S(1)} %get-tuple-element.120), channel_id=1, source_target_pairs={{0,4},{4,8},{8,12},{12,16},{16,20},{20,24},{24,28},{1,5},{5,9},{9,... | collective-permute-start | bytes 1572872 | tf_op jit(solution)/shard_map/ppermute | solution.py:19
  349.3 5.1 %collective-permute-done.38 = f32[2,256,256]{2,1,0:T(8,128)S(1)} collective-permute-done((f32[2,256,256]{2,1,0:T(8,128)S(1)}, f32[2,256,256]{2,1,0:T(8,128)S(1)}, u32[]{:S(2)}, u32[]{:S(2)}) %collective-permute-start.38) | collective-permute-done | bytes 524320 | tf_op jit(solution)/shard_map/ppermute | solution.py:19
  354.5 10.3 %collective-permute-done.37 = f32[2,256,256]{2,1,0:T(8,128)S(1)} collective-permute-done((f32[2,256,256]{2,1,0:T(8,128)S(1)}, f32[2,256,256]{2,1,0:T(8,128)S(1)}, u32[]{:S(2)}, u32[]{:S(2)}) %collective-permute-start.37) | collective-permute-done | bytes 524320 | tf_op jit(solution)/shard_map/ppermute | solution.py:19
  (215 shorter events, 91.1 us)
Async XLA Ops:
  4.7 18.2 %collective-permute-start.2 = (f32[2,256,256]{2,1,0:T(8,128)}, f32[2,256,256]{2,1,0:T(8,128)}, u32[]{:S(2)}, u32[]{:S(2)}) collective-permute-start(f32[2,256,256]{2,1,0:T(8,128)} %get-tuple-element.132), channel_id=1, source_target_pairs={{4,0},{8,4},{12,8},{16,12},{20,16},{24,20},{28,24},{5,1},{9,5},{13... | collective-permute-start | bytes 1572872 | tf_op jit(solution)/shard_map/ppermute | solution.py:19
  6.2 40.9 %collective-permute-start = (f32[2,256,256]{2,1,0:T(8,128)}, f32[2,256,256]{2,1,0:T(8,128)}, u32[]{:S(2)}, u32[]{:S(2)}) collective-permute-start(f32[2,256,256]{2,1,0:T(8,128)} %get-tuple-element.132), channel_id=1, source_target_pairs={{1,0},{2,1},{3,2},{5,4},{6,5},{7,6},{9,8},{10,9},{11,10},{13,12},{... | collective-permute-start | bytes 1572872 | tf_op jit(solution)/shard_map/ppermute | solution.py:19
  8.8 25.3 %collective-permute-start.7 = (f32[2,256,256]{2,1,0:T(8,128)}, f32[2,256,256]{2,1,0:T(8,128)}, u32[]{:S(2)}, u32[]{:S(2)}) collective-permute-start(f32[2,256,256]{2,1,0:T(8,128)} %get-tuple-element.129), channel_id=1, source_target_pairs={{4,0},{8,4},{12,8},{16,12},{20,16},{24,20},{28,24},{5,1},{9,5},{13... | collective-permute-start | bytes 1572872 | tf_op jit(solution)/shard_map/ppermute | solution.py:19
  10.1 34.4 %collective-permute-start.3 = (f32[2,256,256]{2,1,0:T(8,128)}, f32[2,256,256]{2,1,0:T(8,128)}, u32[]{:S(2)}, u32[]{:S(2)}) collective-permute-start(f32[2,256,256]{2,1,0:T(8,128)} %get-tuple-element.130), channel_id=1, source_target_pairs={{4,0},{8,4},{12,8},{16,12},{20,16},{24,20},{28,24},{5,1},{9,5},{13... | collective-permute-start | bytes 1572872 | tf_op jit(solution)/shard_map/ppermute | solution.py:19
  11.4 34.4 %collective-permute-start.1 = (f32[2,256,256]{2,1,0:T(8,128)}, f32[2,256,256]{2,1,0:T(8,128)}, u32[]{:S(2)}, u32[]{:S(2)}) collective-permute-start(f32[2,256,256]{2,1,0:T(8,128)} %get-tuple-element.131), channel_id=1, source_target_pairs={{1,0},{2,1},{3,2},{5,4},{6,5},{7,6},{9,8},{10,9},{11,10},{13,12},{... | collective-permute-start | bytes 1572872 | tf_op jit(solution)/shard_map/ppermute | solution.py:19
  22.9 25.5 %collective-permute-start.4 = (f32[2,256,256]{2,1,0:T(8,128)}, f32[2,256,256]{2,1,0:T(8,128)}, u32[]{:S(2)}, u32[]{:S(2)}) collective-permute-start(f32[2,256,256]{2,1,0:T(8,128)} %collective-permute-done.2.refs_11_), channel_id=1, source_target_pairs={{1,0},{2,1},{3,2},{5,4},{6,5},{7,6},{9,8},{10,9},{11,10},{13,12},{... | collective-permute-start | bytes 1572872 | tf_op jit(solution)/shard_map/ppermute | solution.py:19
  34.1 26.3 %collective-permute-start.5 = (f32[2,256,256]{2,1,0:T(8,128)}, f32[2,256,256]{2,1,0:T(8,128)}, u32[]{:S(2)}, u32[]{:S(2)}) collective-permute-start(f32[2,256,256]{2,1,0:T(8,128)} %get-tuple-element.129), channel_id=1, source_target_pairs={{1,0},{2,1},{3,2},{5,4},{6,5},{7,6},{9,8},{10,9},{11,10},{13,12},{... | collective-permute-start | bytes 1572872 | tf_op jit(solution)/shard_map/ppermute | solution.py:19
  44.5 15.9 %collective-permute-start.8 = (f32[2,256,256]{2,1,0:T(8,128)}, f32[2,256,256]{2,1,0:T(8,128)}, u32[]{:S(2)}, u32[]{:S(2)}) collective-permute-start(f32[2,256,256]{2,1,0:T(8,128)} %get-tuple-element.127), channel_id=1, source_target_pairs={{4,0},{8,4},{12,8},{16,12},{20,16},{24,20},{28,24},{5,1},{9,5},{13... | collective-permute-start | bytes 1572872 | tf_op jit(solution)/shard_map/ppermute | solution.py:19
  45.8 14.6 %collective-permute-start.6 = (f32[2,256,256]{2,1,0:T(8,128)}, f32[2,256,256]{2,1,0:T(8,128)}, u32[]{:S(2)}, u32[]{:S(2)}) collective-permute-start(f32[2,256,256]{2,1,0:T(8,128)} %get-tuple-element.128), channel_id=1, source_target_pairs={{1,0},{2,1},{3,2},{5,4},{6,5},{7,6},{9,8},{10,9},{11,10},{13,12},{... | collective-permute-start | bytes 1572872 | tf_op jit(solution)/shard_map/ppermute | solution.py:19
  47.1 13.3 %collective-permute-start.9 = (f32[2,256,256]{2,1,0:T(8,128)}, f32[2,256,256]{2,1,0:T(8,128)}, u32[]{:S(2)}, u32[]{:S(2)}) collective-permute-start(f32[2,256,256]{2,1,0:T(8,128)} %collective-permute-done.7.refs_14_), channel_id=1, source_target_pairs={{1,0},{2,1},{3,2},{5,4},{6,5},{7,6},{9,8},{10,9},{11,10},{13,12},{... | collective-permute-start | bytes 1572872 | tf_op jit(solution)/shard_map/ppermute | solution.py:19
  77.3 14.2 %collective-permute-start.10 = (f32[3,128,256]{2,1,0:T(8,128)S(1)}, f32[3,128,256]{2,1,0:T(8,128)}, u32[]{:S(2)}, u32[]{:S(2)}) collective-permute-start(f32[3,128,256]{2,1,0:T(8,128)S(1)} %slice_select_fusion.1), channel_id=1, source_target_pairs={{0,1},{1,0},{2,3},{3,2},{4,5},{5,4},{6,7},{7,6},{8,9},{9,8},{10,11... | collective-permute-start | bytes 1179656 | tf_op jit(solution)/shard_map/ppermute | solution.py:24
  114.9 14.1 %collective-permute-start.21 = (f32[2,2,256,256]{3,2,1,0:T(8,128)}, f32[2,2,256,256]{3,2,1,0:T(8,128)S(1)}, u32[]{:S(2)}, u32[]{:S(2)}) collective-permute-start(f32[2,2,256,256]{3,2,1,0:T(8,128)} %get-tuple-element.70), channel_id=1, source_target_pairs={{0,1},{1,2},{2,3},{4,5},{5,6},{6,7},{8,9},{9,10},{10,11},{12,13},{... | collective-permute-start | bytes 3145736 | tf_op jit(solution)/shard_map/ppermute | solution.py:19
  116.2 39.1 %collective-permute-start.20 = (f32[2,2,512,256]{3,2,1,0:T(8,128)}, f32[2,2,512,256]{3,2,1,0:T(8,128)S(1)}, u32[]{:S(2)}, u32[]{:S(2)}) collective-permute-start(f32[2,2,512,256]{3,2,1,0:T(8,128)} %get-tuple-element.66), channel_id=1, source_target_pairs={{0,1},{1,2},{2,3},{4,5},{5,6},{6,7},{8,9},{9,10},{10,11},{12,13},{... | collective-permute-start | bytes 6291464 | tf_op jit(solution)/shard_map/ppermute | solution.py:19
  120.1 33.4 %collective-permute-start.19 = (f32[2,2,256,256]{3,2,1,0:T(8,128)}, f32[2,2,256,256]{3,2,1,0:T(8,128)S(1)}, u32[]{:S(2)}, u32[]{:S(2)}) collective-permute-start(f32[2,2,256,256]{3,2,1,0:T(8,128)} %get-tuple-element.63), channel_id=1, source_target_pairs={{0,4},{4,8},{8,12},{12,16},{16,20},{20,24},{24,28},{1,5},{5,9},{9,... | collective-permute-start | bytes 3145736 | tf_op jit(solution)/shard_map/ppermute | solution.py:19
  128.8 47.1 %collective-permute-start.17 = (f32[2,64,256]{2,1,0:T(8,128)S(1)}, f32[2,64,256]{2,1,0:T(8,128)S(1)}, u32[]{:S(2)}, u32[]{:S(2)}) collective-permute-start(f32[2,64,256]{2,1,0:T(8,128)S(1)} %pad_maximum_fusion.4), channel_id=1, source_target_pairs={{0,2},{1,3},{2,0},{3,1},{4,6},{5,7},{6,4},{7,5},{8,10},{9,11},{10,... | collective-permute-start | bytes 393224 | tf_op jit(solution)/shard_map/ppermute | solution.py:24
  129.1 34.7 %collective-permute-start.28 = (f32[2,256,256]{2,1,0:T(8,128)S(1)}, f32[2,256,256]{2,1,0:T(8,128)S(1)}, u32[]{:S(2)}, u32[]{:S(2)}) collective-permute-start(f32[2,256,256]{2,1,0:T(8,128)S(1)} %get-tuple-element.123), channel_id=1, source_target_pairs={{0,4},{4,8},{8,12},{12,16},{16,20},{20,24},{24,28},{1,5},{5,9},{9,... | collective-permute-start | bytes 1572872 | tf_op jit(solution)/shard_map/ppermute | solution.py:19
  151.5 21.3 %collective-permute-start.22 = (f32[2,256,256]{2,1,0:T(8,128)S(1)}, f32[2,256,256]{2,1,0:T(8,128)S(1)}, u32[]{:S(2)}, u32[]{:S(2)}) collective-permute-start(f32[2,256,256]{2,1,0:T(8,128)S(1)} %get-tuple-element.124), channel_id=1, source_target_pairs={{0,4},{4,8},{8,12},{12,16},{16,20},{20,24},{24,28},{1,5},{5,9},{9,... | collective-permute-start | bytes 1572872 | tf_op jit(solution)/shard_map/ppermute | solution.py:19
  174.6 17.1 %collective-permute-start.25 = (f32[2,256,256]{2,1,0:T(8,128)S(1)}, f32[2,256,256]{2,1,0:T(8,128)S(1)}, u32[]{:S(2)}, u32[]{:S(2)}) collective-permute-start(f32[2,256,256]{2,1,0:T(8,128)S(1)} %get-tuple-element.71.refs_8_), channel_id=1, source_target_pairs={{4,0},{8,4},{12,8},{16,12},{20,16},{24,20},{28,24},{5,1},{9,5},{13... | collective-permute-start | bytes 1572872 | tf_op jit(solution)/shard_map/ppermute | solution.py:19
  176.0 26.9 %collective-permute-start.26 = (f32[2,256,256]{2,1,0:T(8,128)S(1)}, f32[2,256,256]{2,1,0:T(8,128)S(1)}, u32[]{:S(2)}, u32[]{:S(2)}) collective-permute-start(f32[2,256,256]{2,1,0:T(8,128)S(1)} %get-tuple-element.72.refs_9_), channel_id=1, source_target_pairs={{4,0},{8,4},{12,8},{16,12},{20,16},{24,20},{28,24},{5,1},{9,5},{13... | collective-permute-start | bytes 1572872 | tf_op jit(solution)/shard_map/ppermute | solution.py:19
  177.3 26.9 %collective-permute-start.23 = (f32[2,256,256]{2,1,0:T(8,128)S(1)}, f32[2,256,256]{2,1,0:T(8,128)S(1)}, u32[]{:S(2)}, u32[]{:S(2)}) collective-permute-start(f32[2,256,256]{2,1,0:T(8,128)S(1)} %get-tuple-element.71.refs_8_), channel_id=1, source_target_pairs={{1,0},{2,1},{3,2},{5,4},{6,5},{7,6},{9,8},{10,9},{11,10},{13,12},{... | collective-permute-start | bytes 1572872 | tf_op jit(solution)/shard_map/ppermute | solution.py:19
  178.6 35.7 %collective-permute-start.31 = (f32[2,256,256]{2,1,0:T(8,128)}, f32[2,256,256]{2,1,0:T(8,128)}, u32[]{:S(2)}, u32[]{:S(2)}) collective-permute-start(f32[2,256,256]{2,1,0:T(8,128)} %get-tuple-element.79.refs_11_), channel_id=1, source_target_pairs={{4,0},{8,4},{12,8},{16,12},{20,16},{24,20},{28,24},{5,1},{9,5},{13... | collective-permute-start | bytes 1572872 | tf_op jit(solution)/shard_map/ppermute | solution.py:19
  179.9 35.7 %collective-permute-start.24 = (f32[2,256,256]{2,1,0:T(8,128)S(1)}, f32[2,256,256]{2,1,0:T(8,128)S(1)}, u32[]{:S(2)}, u32[]{:S(2)}) collective-permute-start(f32[2,256,256]{2,1,0:T(8,128)S(1)} %get-tuple-element.73.refs_10_), channel_id=1, source_target_pairs={{1,0},{2,1},{3,2},{5,4},{6,5},{7,6},{9,8},{10,9},{11,10},{13,12},{... | collective-permute-start | bytes 1572872 | tf_op jit(solution)/shard_map/ppermute | solution.py:19
  191.7 25.2 %collective-permute-start.27 = (f32[2,256,256]{2,1,0:T(8,128)S(1)}, f32[2,256,256]{2,1,0:T(8,128)S(1)}, u32[]{:S(2)}, u32[]{:S(2)}) collective-permute-start(f32[2,256,256]{2,1,0:T(8,128)S(1)} %collective-permute-done.25.refs_14_), channel_id=1, source_target_pairs={{1,0},{2,1},{3,2},{5,4},{6,5},{7,6},{9,8},{10,9},{11,10},{13,12},{... | collective-permute-start | bytes 1572872 | tf_op jit(solution)/shard_map/ppermute | solution.py:19
  203.0 23.0 %collective-permute-start.32 = (f32[2,256,256]{2,1,0:T(8,128)}, f32[2,256,256]{2,1,0:T(8,128)}, u32[]{:S(2)}, u32[]{:S(2)}) collective-permute-start(f32[2,256,256]{2,1,0:T(8,128)} %get-tuple-element.80.refs_12_), channel_id=1, source_target_pairs={{4,0},{8,4},{12,8},{16,12},{20,16},{24,20},{28,24},{5,1},{9,5},{13... | collective-permute-start | bytes 1572872 | tf_op jit(solution)/shard_map/ppermute | solution.py:19
  204.3 21.8 %collective-permute-start.29 = (f32[2,256,256]{2,1,0:T(8,128)}, f32[2,256,256]{2,1,0:T(8,128)}, u32[]{:S(2)}, u32[]{:S(2)}) collective-permute-start(f32[2,256,256]{2,1,0:T(8,128)} %get-tuple-element.79.refs_11_), channel_id=1, source_target_pairs={{1,0},{2,1},{3,2},{5,4},{6,5},{7,6},{9,8},{10,9},{11,10},{13,12},{... | collective-permute-start | bytes 1572872 | tf_op jit(solution)/shard_map/ppermute | solution.py:19
  247.9 22.3 %collective-permute-start.40 = (f32[3,64,256]{2,1,0:T(8,128)S(1)}, f32[3,64,256]{2,1,0:T(8,128)S(1)}, u32[]{:S(2)}, u32[]{:S(2)}) collective-permute-start(f32[3,64,256]{2,1,0:T(8,128)S(1)} %slice_select_fusion.3), channel_id=1, source_target_pairs={{0,2},{1,3},{2,0},{3,1},{4,6},{5,7},{6,4},{7,5},{8,10},{9,11},{10,... | collective-permute-start | bytes 589832 | tf_op jit(solution)/shard_map/ppermute | solution.py:24
  291.9 44.7 %collective-permute-start.34 = (f32[2,2,256,256]{3,2,1,0:T(8,128)S(1)}, f32[2,2,256,256]{3,2,1,0:T(8,128)S(1)}, u32[]{:S(2)}, u32[]{:S(2)}) collective-permute-start(f32[2,2,256,256]{3,2,1,0:T(8,128)S(1)} %copy-done.36), channel_id=1, source_target_pairs={{0,4},{4,8},{8,12},{12,16},{16,20},{20,24},{24,28},{1,5},{5,9},{9,... | collective-permute-start | bytes 3145736 | tf_op jit(solution)/shard_map/ppermute | solution.py:19
  295.9 42.8 %collective-permute-start.36 = (f32[2,2,256,256]{3,2,1,0:T(8,128)S(1)}, f32[2,2,256,256]{3,2,1,0:T(8,128)S(1)}, u32[]{:S(2)}, u32[]{:S(2)}) collective-permute-start(f32[2,2,256,256]{3,2,1,0:T(8,128)S(1)} %copy-done.35), channel_id=1, source_target_pairs={{0,1},{1,2},{2,3},{4,5},{5,6},{6,7},{8,9},{9,10},{10,11},{12,13},{... | collective-permute-start | bytes 3145736 | tf_op jit(solution)/shard_map/ppermute | solution.py:19
  297.3 50.0 %collective-permute-start.35 = (f32[2,2,512,256]{3,2,1,0:T(8,128)S(1)}, f32[2,2,512,256]{3,2,1,0:T(8,128)S(1)}, u32[]{:S(2)}, u32[]{:S(2)}) collective-permute-start(f32[2,2,512,256]{3,2,1,0:T(8,128)S(1)} %copy-done.34), channel_id=1, source_target_pairs={{0,1},{1,2},{2,3},{4,5},{5,6},{6,7},{8,9},{9,10},{10,11},{12,13},{... | collective-permute-start | bytes 6291464 | tf_op jit(solution)/shard_map/ppermute | solution.py:19
  307.1 39.3 %collective-permute-start.47 = (f32[2,128,256]{2,1,0:T(8,128)S(1)}, f32[2,128,256]{2,1,0:T(8,128)S(1)}, u32[]{:S(2)}, u32[]{:S(2)}) collective-permute-start(f32[2,128,256]{2,1,0:T(8,128)S(1)} %pad_maximum_fusion.3), channel_id=1, source_target_pairs={{0,1},{1,0},{2,3},{3,2},{4,5},{5,4},{6,7},{7,6},{8,9},{9,8},{10,11... | collective-permute-start | bytes 786440 | tf_op jit(solution)/shard_map/ppermute | solution.py:24
  338.9 15.6 %collective-permute-start.38 = (f32[2,256,256]{2,1,0:T(8,128)S(1)}, f32[2,256,256]{2,1,0:T(8,128)S(1)}, u32[]{:S(2)}, u32[]{:S(2)}) collective-permute-start(f32[2,256,256]{2,1,0:T(8,128)S(1)} %get-tuple-element.119), channel_id=1, source_target_pairs={{0,4},{4,8},{8,12},{12,16},{16,20},{20,24},{24,28},{1,5},{5,9},{9,... | collective-permute-start | bytes 1572872 | tf_op jit(solution)/shard_map/ppermute | solution.py:19
  342.2 22.6 %collective-permute-start.37 = (f32[2,256,256]{2,1,0:T(8,128)S(1)}, f32[2,256,256]{2,1,0:T(8,128)S(1)}, u32[]{:S(2)}, u32[]{:S(2)}) collective-permute-start(f32[2,256,256]{2,1,0:T(8,128)S(1)} %get-tuple-element.120), channel_id=1, source_target_pairs={{0,4},{4,8},{8,12},{12,16},{16,20},{20,24},{24,28},{1,5},{5,9},{9,... | collective-permute-start | bytes 1572872 | tf_op jit(solution)/shard_map/ppermute | solution.py:19
  (55 other events, 1130.3 us)
